TPU v7x, 256 devices: a whole 4x4x8 slice. The times are simulated.
256 devices in a mesh: grp: 2 (over z_hi), gy: 4 (over z_lo), gz: 32 (over x, y, core).
Axes of the slice: x: 4, y: 4, z: 8 (z_hi: 2, z_lo: 4; z = z_hi * 4 + z_lo), core: 2. Of those that a mesh axis runs over, the one named last changes fastest.
Arguments:
- vorticity: float32 [2, 3, 256, 256, 256], P('grp', None, 'gz', 'gy'), may hold values from -6 to 6
- wind: float32 [2, 3], P('grp'), may hold values from 0.5 to 1.2
Outputs:
- new_vorticity: float32 [2, 3, 256, 256, 256], P('grp', None, 'gz', 'gy')
- velocity: float32 [2, 3, 256, 256, 256], P('grp', None, 'gz', 'gy')
All inputs are finite; a program needn't handle non-finite values.
Results may differ from a plain program's by a relative error of at most 0.0003.
Values sent between devices are 32-bit elements; how exact they have to be, the bound alone decides.
No kernel may reach another device: no remote copies, remote signals or barrier semaphores. Data moves between devices by JAX's collectives and lax.ppermute only.
A program may use at most 128 MiB of HBM per device.

v0:
```python
import math

import jax
import jax.numpy as jnp
import numpy as np
from jax import lax
from jax.experimental import pallas as pl
from jax.experimental.pallas import tpu as pltpu
from jax.sharding import PartitionSpec as P

TIME_STEP = 0.4
BF16 = jnp.bfloat16
F32 = jnp.float32
VMEM_LIMIT = 60 * 1024 * 1024


def angles(count):
    index = np.arange(count)
    return (index[:, None] * index[None, :] % count) * (2.0 * math.pi / count)


def halves(table):
    table = np.asarray(table, np.float32)
    high = table.astype(BF16)
    low = (table - high.astype(np.float32)).astype(BF16)
    return high, low


def left_table(table):
    high, low = halves(table)
    return np.concatenate([high, high, low], 1)


def right_table(table):
    high, low = halves(table)
    return np.concatenate([high, high, low], 0)


def split(value):
    high = value.astype(BF16)
    low = (value - high.astype(F32)).astype(BF16)
    return high, low


def streamwise_tables(count):
    half = count // 2
    cosine, sine = np.cos(angles(count)), np.sin(angles(count))
    alternate = 1.0 - 2.0 * (np.arange(count) % 2)
    forward = np.concatenate([cosine[:half], alternate[None], -sine[1:half]], 0)
    scale = np.full((half, 1), 2.0)
    scale[0] = 1.0
    backward = np.concatenate([scale * cosine[:half], alternate[None], -2.0 * sine[1:half]], 0)
    return forward, backward / count


def vertical_table(count, blocks):
    local = count // blocks
    z = np.arange(blocks)[None, :, None] * local + np.arange(local // 2)[None, None, :] * 2
    z = z + np.arange(2)[:, None, None]
    phase = (np.arange(count)[:, None, None, None] * z[None] % count) * (2.0 * math.pi / count)
    cosine, sine = np.cos(phase), np.sin(phase)
    real = np.stack([cosine, sine], 3)
    imag = np.stack([-sine, cosine], 3)
    return np.stack([real, imag]).reshape(2 * count, 2 * count)


def streamwise_forward(field_ref, table_ref, out_ref):
    comps, local_z, local_y, count = field_ref.shape
    rows = local_z * local_y
    table = table_ref[...]
    for c in range(comps):
        value = field_ref[c].reshape(rows, count)
        high, low = split(value)
        stacked = jnp.concatenate([high, low, high], 1)
        result = lax.dot_general(
            table, stacked, (((1,), (1,)), ((), ())), preferred_element_type=F32
        )
        for part in range(2):
            for k in range(0, count // 2, 8):
                for a in range(rows // 128):
                    top = part * (count // 2) + k
                    out_ref[pl.ds(k * 24 + c * 8 + part * 4 + a, 8, stride=24), :] = result[
                        top : top + 8, a * 128 : (a + 1) * 128
                    ]


def product(left, right):
    return jnp.dot(left, right, preferred_element_type=F32)


def left_product(table, value):
    high, low = split(value)
    return product(table, jnp.concatenate([high, low, high], 0))


def right_product(value, table):
    high, low = split(value)
    return product(jnp.concatenate([high, low, high], 1), table)


def signed_waves(index, count, odd):
    signed = jnp.where(index < count // 2, index, index - count)
    if odd:
        signed = jnp.where(index == count // 2, 0, signed)
    return signed.astype(F32) * (2.0 * math.pi / count)


def plane_kernel(owner_ref, in_ref, z_ref, y_ref, back_ref, flip_ref, out_ref, plain_ref):
    n = y_ref.shape[1] // 2
    owner = owner_ref[0]
    is_packed = owner == 0
    low_lanes = lax.broadcasted_iota(jnp.int32, (n, 128), 1) < 64
    row = lax.broadcasted_iota(jnp.int32, (n, n), 0)
    col = lax.broadcasted_iota(jnp.int32, (n, n), 1)
    wave_x = owner.astype(F32) * (2.0 * math.pi / n)
    wave_z = signed_waves(row, n, False)
    wave_y = signed_waves(col, n, False)
    curl_z = signed_waves(row, n, True)
    curl_y = signed_waves(col, n, True)
    plane = wave_y * wave_y + wave_z * wave_z
    squared = plane + wave_x * wave_x
    scale = jnp.where(squared > 0, 1.0 / jnp.where(squared > 0, squared, 1.0), 0.0)
    top_scale = 1.0 / (plane + math.pi * math.pi)
    sigma = jnp.where(is_packed, 0.5 * (scale + top_scale), scale)
    delta = 0.5 * (scale - top_scale)
    for c in range(3):
        blocks = [
            in_ref[32 * g : 32 * g + 32, 8 * c : 8 * c + 8, :].reshape(n, 128) for g in range(4)
        ]
        tops, bottoms = [], []
        for g in (0, 2):
            first, second = blocks[g], blocks[g + 1]
            tops.append(jnp.where(low_lanes, first, pltpu.roll(second, 64, 1)))
            bottoms.append(jnp.where(low_lanes, pltpu.roll(first, 64, 1), second))
        value = jnp.concatenate(
            [jnp.concatenate(tops, 1), jnp.concatenate(bottoms, 1)], 0
        )
        value = left_product(z_ref[...], value)
        value = right_product(value, y_ref[...])
        real_cos, real_sin = value[:n, :n], value[:n, n:]
        imag_cos, imag_sin = value[n:, :n], value[n:, n:]
        plain_ref[c, :n, :] = (real_cos + imag_sin) * sigma
        plain_ref[c, n:, :] = (imag_cos - real_sin) * sigma

        @pl.when(is_packed)
        def _():
            turned = jnp.concatenate([real_cos - imag_sin, imag_cos + real_sin], 1)
            high, low = split(turned)
            mirror = product(flip_ref[...], high) + product(flip_ref[...], low)
            plain_ref[c, :n, :] += mirror[:, :n] * delta
            plain_ref[c, n:, :] -= mirror[:, n:] * delta

    for c in range(3):
        if c == 0:
            def cross(part):
                return curl_y * plain_ref[2, part] - curl_z * plain_ref[1, part]
        elif c == 1:
            def cross(part):
                return curl_z * plain_ref[0, part] - wave_x * plain_ref[2, part]
        else:
            def cross(part):
                return wave_x * plain_ref[1, part] - curl_y * plain_ref[0, part]
        value = jnp.concatenate([-cross(slice(n, 2 * n)), cross(slice(0, n))], 0)
        value = right_product(value, y_ref[...])
        real = value[:n, :n] - value[n:, n:]
        imag = value[n:, :n] + value[:n, n:]
        value = left_product(back_ref[...], jnp.concatenate([real, imag], 0))
        for pair in range(2):
            top = value[:n, 128 * pair : 128 * pair + 128]
            bottom = value[n:, 128 * pair : 128 * pair + 128]
            first = jnp.where(low_lanes, top, pltpu.roll(bottom, 64, 1))
            second = jnp.where(low_lanes, pltpu.roll(top, 64, 1), bottom)
            for g, block in ((2 * pair, first), (2 * pair + 1, second)):
                out_ref[32 * g : 32 * g + 32, 8 * c : 8 * c + 8, :] = block.reshape(32, 8, 128)


def streamwise_backward(in_ref, table_ref, drift_ref, out_ref):
    comps, local_z, local_y, count = out_ref.shape
    for c in range(comps):
        parts = []
        for part in range(2):
            chunks = [
                in_ref[pl.ds(c * 8 + part * 4 + a, count // 2, stride=24), :] for a in range(4)
            ]
            parts.append(jnp.concatenate(chunks, 1))
        value = jnp.concatenate(parts, 0).T
        result = right_product(value, table_ref[...]) + drift_ref[0, c]
        out_ref[c] = result.reshape(local_z, local_y, count)


def call(kernel, shape, args, smem=(), scratch=()):
    specs = [
        pl.BlockSpec(memory_space=pltpu.SMEM if i in smem else pltpu.VMEM)
        for i in range(len(args))
    ]
    return pl.pallas_call(
        kernel,
        out_shape=jax.ShapeDtypeStruct(shape, F32),
        in_specs=specs,
        out_specs=pl.BlockSpec(memory_space=pltpu.VMEM),
        scratch_shapes=list(scratch),
        compiler_params=pltpu.CompilerParams(vmem_limit_bytes=VMEM_LIMIT),
    )(*args)


def forward_lines(field):
    count = field.shape[3]
    forward, _ = streamwise_tables(count)
    table = jnp.asarray(left_table(forward))
    return call(streamwise_forward, (count // 2 * 24, 128), (field, table))


def solve_plane(spectrum, owner, count, blocks):
    vertical = vertical_table(count, blocks)
    phase = angles(count)
    lateral = np.concatenate([np.cos(phase), np.sin(phase)], 1)
    flip = np.zeros((count, count), np.float32)
    flip[np.arange(count), -np.arange(count) % count] = 1.0
    args = (
        owner.reshape(1),
        spectrum,
        jnp.asarray(left_table(vertical)),
        jnp.asarray(right_table(lateral)),
        jnp.asarray(left_table(vertical.T / (count * count))),
        jnp.asarray(flip.astype(BF16)),
    )
    scratch = (pltpu.VMEM((3, 2 * count, count), F32),)
    return call(plane_kernel, spectrum.shape, args, smem=(0,), scratch=scratch)


def backward_lines(spectrum, drift, shape):
    _, backward = streamwise_tables(shape[3])
    table = jnp.asarray(right_table(backward))
    return call(streamwise_backward, shape, (spectrum, table, drift), smem=(2,))


def shifted(value, axis, steps):
    count = lax.axis_size(axis)
    initial, last = (max(0, -steps), min(count, count - steps))
    return lax.ppermute(value, axis, [(source, source + steps) for source in range(initial, last)])


def padded(array, sides, width):
    edges = {}
    for axis, dim in sides:
        devices, length = (lax.axis_size(axis), array.shape[dim])
        up = [(i, (i + 1) % devices) for i in range(devices)]
        last = lax.slice_in_dim(array, length - width, length, axis=dim)
        initial = lax.slice_in_dim(array, 0, width, axis=dim)
        edges[dim] = (
            lax.ppermute(last, axis, up),
            lax.ppermute(initial, axis, [(b, a) for a, b in up]),
        )
    done = []
    for _, dim in sides:
        low, high = edges[dim]
        around = [(width, width) if d in done else (0, 0) for d in range(array.ndim)]
        array = jnp.concatenate([jnp.pad(low, around), array, jnp.pad(high, around)], axis=dim)
        done.append(dim)
    return array


def extended_2(cells, sides, width):
    for axis, dim in sides:
        count = lax.axis_size(axis)
        head = lax.slice_in_dim(cells, 0, width, axis=dim)
        tail = lax.slice_in_dim(cells, cells.shape[dim] - width, cells.shape[dim], axis=dim)
        cells = jnp.concatenate(
            [
                lax.ppermute(tail, axis, [(i, (i + 1) % count) for i in range(count)]),
                cells,
                lax.ppermute(head, axis, [((i + 1) % count, i) for i in range(count)]),
            ],
            axis=dim,
        )
    return cells


def kernel_weight(offset):
    mag = jnp.abs(offset)
    inner = 1.0 - 2.5 * mag * mag + 1.5 * mag * mag * mag
    outer = 0.5 * (2.0 - mag) * (2.0 - mag) * (1.0 - mag)
    return jnp.where(mag < 1.0, inner, jnp.where(mag < 2.0, outer, 0.0 * mag))


def body(vorticity, wind):
    is_wake = lax.axis_index("grp") == 1
    field = vorticity[0]
    count_x = field.shape[3]
    size_gz = lax.axis_size("gz")
    groups = lax.axis_size("gy") * size_gz
    owner = lax.axis_index("gy") * size_gz + lax.axis_index("gz")
    axes = ("gy", "gz")
    spectrum = forward_lines(field).reshape(groups, 24, 128)
    spectrum = lax.all_to_all(spectrum, axes, split_axis=0, concat_axis=0, tiled=True)
    spectrum = solve_plane(spectrum, owner, count_x, size_gz)
    spectrum = lax.all_to_all(spectrum, axes, split_axis=0, concat_axis=0, tiled=True)
    velocity = backward_lines(spectrum.reshape(groups * 24, 128), wind, field.shape)
    planes = shifted(velocity[..., count_x - 2 :], "grp", 1)
    rimmed = padded(velocity, (("gz", 1), ("gy", 2)), 1)
    grad_z = (rimmed[:, 2:, 1:-1, :] - rimmed[:, :-2, 1:-1, :]) * 0.5
    grad_y = (rimmed[:, 1:-1, 2:, :] - rimmed[:, 1:-1, :-2, :]) * 0.5
    left_side = jnp.where(is_wake, planes[..., 1:], velocity[..., count_x - 1 :])
    right_side = jnp.where(is_wake, velocity[..., count_x - 1 :], velocity[..., :1])
    extended = jnp.concatenate([left_side, velocity, right_side], -1)
    grad_x = (extended[..., 2:] - extended[..., :-2]) * 0.5
    strength = field + TIME_STEP * (field[0:1] * grad_x + field[1:2] * grad_y + field[2:3] * grad_z)
    ghost = shifted(strength[..., count_x - 2 :], "grp", 1)
    shift_x = TIME_STEP * velocity[0]
    left_q = jnp.where(is_wake, ghost, strength[..., count_x - 2 :])
    left_d = jnp.where(is_wake, TIME_STEP * planes[0], shift_x[..., count_x - 2 :])
    right_q = jnp.where(is_wake, 0.0, strength[..., :2])
    right_d = jnp.where(is_wake, 0.0, shift_x[..., :2])
    q_ext = jnp.concatenate([left_q, strength, right_q], -1)
    d_ext = jnp.concatenate([left_d, shift_x, right_d], -1)
    moved = jnp.zeros_like(strength)
    for offset in range(-2, 3):
        start = 2 - offset
        moved = moved + q_ext[..., start : start + count_x] * kernel_weight(
            offset - d_ext[..., start : start + count_x]
        )
    packed = jnp.concatenate([moved, TIME_STEP * velocity[1:2]], 0)
    rim_rows = extended_2(packed, (("gy", 2),), 2)
    width_y = moved.shape[2]
    lateral = jnp.zeros_like(moved)
    for offset in range(-2, 3):
        start = 2 - offset
        lateral = lateral + rim_rows[:3, :, start : start + width_y, :] * kernel_weight(
            offset - rim_rows[3:4, :, start : start + width_y, :]
        )
    packed = jnp.concatenate([lateral, TIME_STEP * velocity[2:3]], 0)
    rim_cols = extended_2(packed, (("gz", 1),), 2)
    width_z = moved.shape[1]
    result = jnp.zeros_like(moved)
    for offset in range(-2, 3):
        start = 2 - offset
        result = result + rim_cols[:3, start : start + width_z, :, :] * kernel_weight(
            offset - rim_cols[3:4, start : start + width_z, :, :]
        )
    return (result[None], velocity[None])


def solution(mesh):
    return jax.shard_map(
        body,
        mesh=mesh,
        in_specs=(P("grp", None, "gz", "gy", None), P("grp", None)),
        out_specs=(P("grp", None, "gz", "gy", None), P("grp", None, "gz", "gy", None)),
        check_vma=False,
    )
```

profile of v0, /device:TPU:31, one launch (start us, length us, event | category | flops | bytes accessed | tf_op | source)
XLA Modules:
  0.0 184.9 jit_solution(6166299910941745534)
XLA Ops:
  0.6 3.5 %shard_map.95 = f32[3072,128]{1,0:T(8,128)} custom-call(f32[3,8,64,256]{3,2,1,0:T(8,128)} %bitcast.41, bf16[256,768]{1,0:T(8,128)(2,1)} %constant.14.clone.table_ref), custom_call_target="tpu_custom_call" | custom-call | tf_op jit(solution)/shard_map/pallas_call | solution.py:196
  4.1 12.8 %all-to-all-start = ((f32[128,24,128]{2,1,0:T(8,128)}), f32[128,24,128]{2,1,0:T(8,128)S(1)}, u32[]{:S(2)}, u32[]{:S(2)}) async-start(f32[128,24,128]{2,1,0:T(8,128)} %bitcast.42), calls=%async_computation | async-start | bytes 3145728 | tf_op jit(solution)/shard_map/all_to_all | solution.py:295
  16.9 37.0 %all-to-all-done.in_ref = f32[128,24,128]{2,1,0:T(8,128)S(1)} async-done(((f32[128,24,128]{2,1,0:T(8,128)}), f32[128,24,128]{2,1,0:T(8,128)S(1)}, u32[]{:S(2)}, u32[]{:S(2)}) %all-to-all-start) | async-done | bytes 1572896 | tf_op jit(solution)/shard_map/all_to_all | solution.py:295
  53.9 1.1 copy-done.5
  55.1 12.9 %shard_map.96 = f32[128,24,128]{2,1,0:T(8,128)} custom-call(s32[1]{0:T(128)} %bitcast.1.owner_ref, f32[128,24,128]{2,1,0:T(8,128)} %copy-done.5, bf16[512,1536]{1,0:T(8,128)(2,1)} %constant.15.clone.z_ref, bf16[768,512]{1,0:T(8,128)(2,1)} %constant.16.clone.y_ref, bf16[512,1536]{1,0:T(8,128)(2,1)} %constant.17.clone.back_ref, ...), custom_call_target="tpu_custom_call" | custom-call | tf_op jit(solution)/shard_map/pallas_call | solution.py:196
  67.9 11.4 %all-to-all-start.1 = ((f32[128,24,128]{2,1,0:T(8,128)}), f32[128,24,128]{2,1,0:T(8,128)S(1)}, u32[]{:S(2)}, u32[]{:S(2)}) async-start(f32[128,24,128]{2,1,0:T(8,128)} %shard_map.96), calls=%async_computation.1 | async-start | bytes 3145728 | tf_op jit(solution)/shard_map/all_to_all | solution.py:297
  79.4 1.2 multiply_bitcast_fusion.2
  80.6 35.7 %all-to-all-done.1 = f32[128,24,128]{2,1,0:T(8,128)S(1)} async-done(((f32[128,24,128]{2,1,0:T(8,128)}), f32[128,24,128]{2,1,0:T(8,128)S(1)}, u32[]{:S(2)}, u32[]{:S(2)}) %all-to-all-start.1) | async-done | bytes 1572896 | tf_op jit(solution)/shard_map/all_to_all | solution.py:297
  116.3 1.1 copy-done.6
  117.5 3.6 %shard_map.97 = f32[3,8,64,256]{3,2,1,0:T(8,128)} custom-call(f32[3072,128]{1,0:T(8,128)} %bitcast.43, bf16[768,256]{1,0:T(8,128)(2,1)} %constant.19.clone.table_ref, f32[1,3]{1,0:T(1,128)} %drift_ref.1), custom_call_target="tpu_custom_call" | custom-call | tf_op jit(solution)/shard_map/pallas_call | solution.py:196
  121.1 1.9 %fusion.137 = (f32[3,1,64,256]{3,2,1,0:T(8,128)}, f32[3,1,64,256]{3,2,1,0:T(8,128)}) fusion(f32[3,8,64,256]{3,2,1,0:T(8,128)} %shard_map.97), kind=kLoop, calls=%fused_computation.245 | loop fusion | bytes 786432 | tf_op jit(solution)/shard_map/slice | solution.py:249
  123.0 1.4 slice.249
  124.4 1.8 fusion.102
  126.2 0.3 copy.10
  126.5 6.1 %collective-permute-start = (f32[3,8,64,2]{2,1,3,0:T(8,128)S(1)}, f32[3,8,64,2]{2,1,3,0:T(8,128)S(1)}, u32[]{:S(2)}, u32[]{:S(2)}) collective-permute-start(f32[3,8,64,2]{2,1,3,0:T(8,128)S(1)} %copy.10), channel_id=1, source_target_pairs={{0,128},{1,129},{2,130},{3,131},{4,132},{5,133},{6,134},{7,135},{8... | collective-permute-start | bytes 36872 | tf_op jit(solution)/shard_map/ppermute | solution.py:240
  132.7 0.7 collective-permute-start.3
  133.4 0.8 collective-permute-start.4
  134.2 1.8 collective-permute-start.2
  136.1 3.8 %collective-permute-start.1 = (f32[3,1,64,256]{3,2,1,0:T(8,128)}, f32[3,1,64,256]{3,2,1,0:T(8,128)}, u32[]{:S(2)}, u32[]{:S(2)}) collective-permute-start(f32[3,1,64,256]{3,2,1,0:T(8,128)} %get-tuple-element.38), channel_id=1, source_target_pairs={{0,1},{1,2},{2,3},{3,4},{4,5},{5,6},{6,7},{7,8},{8,9},{9,10},{10,1... | collective-permute-start | bytes 589832 | tf_op jit(solution)/shard_map/ppermute | solution.py:251
  139.9 0.0 collective-permute-done
  139.9 0.2 copy.14
  140.1 0.3 copy.11
  140.4 0.0 copy-start.2
  140.4 0.3 slice_select_fusion.1
  140.8 0.9 slice_select_fusion.4
  141.6 0.0 collective-permute-done.3
  141.7 0.0 collective-permute-done.4
  141.7 1.9 %collective-permute-done.2 = f32[3,1,64,256]{3,2,1,0:T(8,128)} collective-permute-done((f32[3,1,64,256]{3,2,1,0:T(8,128)}, f32[3,1,64,256]{3,2,1,0:T(8,128)}, u32[]{:S(2)}, u32[]{:S(2)}) %collective-permute-start.2) | collective-permute-done | bytes 196640 | tf_op jit(solution)/shard_map/ppermute | solution.py:252
  143.6 0.0 collective-permute-done.1
  143.6 3.0 %fusion.23 = f32[3,8,64,256]{3,2,1,0:T(8,128)S(1)} fusion(f32[3,8,64,256]{3,2,1,0:T(8,128)S(1)} %copy-done, f32[3,1,64,256]{3,2,1,0:T(8,128)} %collective-permute-done.1, f32[3,1,64,256]{3,2,1,0:T(8,128)} %collective-permute-done.2, f32[3,8,1,256]{3,2,1,0:T(1,128)S(1)} %collective-permute-done.4, f32[3,8,1,256]{3,2,1,0:T(1,128)S(1)} %collective-permute-done.3, ...), kind=kLoop, calls=%fused_computation.42 | loop fusion | flops 10223616 | bytes 6746112 | tf_op jit(solution)/shard_map/add | solution.py:307
  146.7 0.3 slice.262
  146.9 0.3 copy.12
  147.2 1.3 collective-permute-start.5
  148.5 0.0 copy-done.8
  148.6 0.0 copy-done.19
  148.6 2.8 %fusion.33 = (f32[8,64,256]{2,1,0:T(8,128)}, f32[8,64,256]{2,1,0:T(8,128)}, f32[8,64,256]{2,1,0:T(8,128)}, f32[8,64,256]{2,1,0:T(8,128)}) fusion(f32[8,64,2]{2,1,0:T(8,128)S(1)} %get-tuple-element.45, f32[8,64,256]{2,1,0:T(8,128)S(1)} %copy-done.8, f32[8,64,2]{2,1,0:T(8,128)S(1)} %copy-done.19), kind=kLoop, calls=%fused_computation.115 | loop fusion | flops 10485760 | bytes 2629632 | tf_op jit(solution)/shard_map/jit(_where)/select_n | solution.py:283
  151.4 0.0 collective-permute-done.5
  151.4 0.3 copy.13
  151.7 0.3 slice_select_fusion
  152.1 0.7 copy-done.9
  152.7 0.2 copy-done.10
  152.9 0.2 copy-done.11
  153.1 0.2 copy-done.12
  153.2 0.2 copy-done.13
  153.4 2.6 %fusion.3 = f32[3,8,64,256]{3,2,1,0:T(8,128)S(1)} fusion(f32[3,8,64,2]{3,2,1,0:T(8,128)S(1)} %get-tuple-element.29, f32[3,8,64,256]{3,2,1,0:T(8,128)S(1)} %fusion.23, f32[3,8,64,2]{3,2,1,0:T(8,128)S(1)} %get-tuple-element.28, f32[8,64,256]{2,1,0:T(8,128)S(1)} %copy-done.12, f32[8,64,256]{2,1,0:T(8,128)S(1)} %copy-done.13, f32[8,64,256]{2,1,0:T(8,128)S(1)} %copy-done.9, ...), kind=kLoop, calls=%fused_computation.11 | loop fusion | flops 5111808 | bytes 5791744 | tf_op jit(solution)/shard_map/add | solution.py:319
  156.1 2.6 %collective-permute-start.6 = (f32[4,8,2,256]{3,2,1,0:T(2,128)S(1)}, f32[4,8,2,256]{3,2,1,0:T(2,128)S(1)}, u32[]{:S(2)}, u32[]{:S(2)}) collective-permute-start(f32[4,8,2,256]{3,2,1,0:T(2,128)S(1)} %get-tuple-element.20), channel_id=1, source_target_pairs={{32,0},{64,32},{96,64},{0,96},{33,1},{65,33},{97,65},{1,97},{34,2}... | collective-permute-start | bytes 196616 | tf_op jit(solution)/shard_map/ppermute | solution.py:272
  158.7 0.0 collective-permute-start.7
  158.7 1.8 collective-permute-done.6
  160.5 4.0 %collective-permute-done.7 = f32[4,8,2,256]{3,2,1,0:T(2,128)S(1)} collective-permute-done((f32[4,8,2,256]{3,2,1,0:T(2,128)S(1)}, f32[4,8,2,256]{3,2,1,0:T(2,128)S(1)}, u32[]{:S(2)}, u32[]{:S(2)}) %collective-permute-start.7) | collective-permute-done | bytes 65568 | tf_op jit(solution)/shard_map/ppermute | solution.py:270
  164.6 1.4 fusion.60
  166.0 0.5 pad_maximum_fusion.1
  166.5 0.6 copy-done.15
  167.1 1.0 fusion.13
  168.0 0.1 copy-done.3
  168.1 0.1 pad_maximum_fusion.13
  168.2 0.5 collective-permute-start.8
  168.7 5.2 %collective-permute-start.9 = (f32[4,2,64,256]{3,2,1,0:T(8,128)S(1)}, f32[4,2,64,256]{3,2,1,0:T(8,128)S(1)}, u32[]{:S(2)}, u32[]{:S(2)}) collective-permute-start(f32[4,2,64,256]{3,2,1,0:T(8,128)S(1)} %get-tuple-element.15), channel_id=1, source_target_pairs={{0,1},{1,2},{2,3},{3,4},{4,5},{5,6},{6,7},{7,8},{8,9},{9,10},{10,1... | collective-permute-start | bytes 1572872 | tf_op jit(solution)/shard_map/ppermute | solution.py:270
  173.9 6.8 %collective-permute-done.8 = f32[4,2,64,256]{3,2,1,0:T(8,128)S(1)} collective-permute-done((f32[4,2,64,256]{3,2,1,0:T(8,128)S(1)}, f32[4,2,64,256]{3,2,1,0:T(8,128)S(1)}, u32[]{:S(2)}, u32[]{:S(2)}) %collective-permute-start.8) | collective-permute-done | bytes 524320 | tf_op jit(solution)/shard_map/ppermute | solution.py:272
  180.6 0.0 collective-permute-done.9
  180.6 1.3 fusion.90
  181.9 0.0 copy-start.14
  181.9 0.7 pad_maximum_fusion
  182.6 0.4 copy-done.14
  183.0 1.9 %fusion.9 = f32[1,3,8,64,256]{4,3,2,1,0:T(8,128)} fusion(f32[4,10,64,256]{3,2,1,0:T(8,128)S(1)} %get-tuple-element.13, f32[4,10,64,256]{3,2,1,0:T(8,128)S(1)} %get-tuple-element.12, f32[3,8,64,256]{3,2,1,0:T(8,128)S(1)} %fusion.13, f32[8,64,256]{2,1,0:T(8,128)S(1)} %get-tuple-element.10, f32[8,64,256]{2,1,0:T(8,128)S(1)} %get-tuple-element.11, ...), kind=kLoop, calls=%fused_computation.18 | loop fusion | flops 3538944 | bytes 12058624 | tf_op jit(solution)/shard_map/broadcast_in_dim | solution.py:340
  (30 shorter events, 0.1 us)
Async XLA Ops:
  4.1 49.8 %all-to-all-start = ((f32[128,24,128]{2,1,0:T(8,128)}), f32[128,24,128]{2,1,0:T(8,128)S(1)}, u32[]{:S(2)}, u32[]{:S(2)}) async-start(f32[128,24,128]{2,1,0:T(8,128)} %bitcast.42), calls=%async_computation | async-start | bytes 3145728 | tf_op jit(solution)/shard_map/all_to_all | solution.py:295
  53.9 1.1 copy-start.5
  67.9 11.4 %copy-start.1 = (f32[1,3,8,64,256]{4,3,2,1,0:T(8,128)S(1)}, f32[1,3,8,64,256]{4,3,2,1,0:T(8,128)}, u32[]{:S(2)}) copy-start(f32[1,3,8,64,256]{4,3,2,1,0:T(8,128)} %param.8) | copy-start | bytes 4718596
  67.9 48.4 %all-to-all-start.1 = ((f32[128,24,128]{2,1,0:T(8,128)}), f32[128,24,128]{2,1,0:T(8,128)S(1)}, u32[]{:S(2)}, u32[]{:S(2)}) async-start(f32[128,24,128]{2,1,0:T(8,128)} %shard_map.96), calls=%async_computation.1 | async-start | bytes 3145728 | tf_op jit(solution)/shard_map/all_to_all | solution.py:297
  116.3 1.1 copy-start.6
  121.1 3.3 %copy-start = (f32[3,8,64,256]{3,2,1,0:T(8,128)S(1)}, f32[3,8,64,256]{3,2,1,0:T(8,128)}, u32[]{:S(2)}) copy-start(f32[3,8,64,256]{3,2,1,0:T(8,128)} %shard_map.97) | copy-start | bytes 4718596
  126.2 14.6 %copy-start.7 = (f32[8,64,256]{2,1,0:T(8,128)}, f32[8,64,256]{2,1,0:T(8,128)S(1)}, u32[]{:S(2)}) copy-start(f32[8,64,256]{2,1,0:T(8,128)S(1)} %get-tuple-element.25) | copy-start | bytes 1572868
  126.5 13.4 %collective-permute-start = (f32[3,8,64,2]{2,1,3,0:T(8,128)S(1)}, f32[3,8,64,2]{2,1,3,0:T(8,128)S(1)}, u32[]{:S(2)}, u32[]{:S(2)}) collective-permute-start(f32[3,8,64,2]{2,1,3,0:T(8,128)S(1)} %copy.10), channel_id=1, source_target_pairs={{0,128},{1,129},{2,130},{3,131},{4,132},{5,133},{6,134},{7,135},{8... | collective-permute-start | bytes 36872 | tf_op jit(solution)/shard_map/ppermute | solution.py:240
  132.7 9.0 %collective-permute-start.3 = (f32[3,8,1,256]{3,2,1,0:T(1,128)S(1)}, f32[3,8,1,256]{3,2,1,0:T(1,128)S(1)}, u32[]{:S(2)}, u32[]{:S(2)}) collective-permute-start(f32[3,8,1,256]{3,2,1,0:T(1,128)S(1)} %get-tuple-element.35), channel_id=1, source_target_pairs={{32,0},{64,32},{96,64},{0,96},{33,1},{65,33},{97,65},{1,97},{34,2}... | collective-permute-start | bytes 73736 | tf_op jit(solution)/shard_map/ppermute | solution.py:252
  133.4 8.2 %collective-permute-start.4 = (f32[3,8,1,256]{3,2,1,0:T(1,128)S(1)}, f32[3,8,1,256]{3,2,1,0:T(1,128)S(1)}, u32[]{:S(2)}, u32[]{:S(2)}) collective-permute-start(f32[3,8,1,256]{3,2,1,0:T(1,128)S(1)} %get-tuple-element.36), channel_id=1, source_target_pairs={{0,32},{32,64},{64,96},{96,0},{1,33},{33,65},{65,97},{97,1},{2,34}... | collective-permute-start | bytes 73736 | tf_op jit(solution)/shard_map/ppermute | solution.py:251
  134.2 9.3 %collective-permute-start.2 = (f32[3,1,64,256]{3,2,1,0:T(8,128)}, f32[3,1,64,256]{3,2,1,0:T(8,128)}, u32[]{:S(2)}, u32[]{:S(2)}) collective-permute-start(f32[3,1,64,256]{3,2,1,0:T(8,128)} %get-tuple-element.37), channel_id=1, source_target_pairs={{1,0},{2,1},{3,2},{4,3},{5,4},{6,5},{7,6},{8,7},{9,8},{10,9},{11,1... | collective-permute-start | bytes 589832 | tf_op jit(solution)/shard_map/ppermute | solution.py:252
  136.1 7.5 %collective-permute-start.1 = (f32[3,1,64,256]{3,2,1,0:T(8,128)}, f32[3,1,64,256]{3,2,1,0:T(8,128)}, u32[]{:S(2)}, u32[]{:S(2)}) collective-permute-start(f32[3,1,64,256]{3,2,1,0:T(8,128)} %get-tuple-element.38), channel_id=1, source_target_pairs={{0,1},{1,2},{2,3},{3,4},{4,5},{5,6},{6,7},{7,8},{8,9},{9,10},{10,1... | collective-permute-start | bytes 589832 | tf_op jit(solution)/shard_map/ppermute | solution.py:251
  140.4 3.2 %copy-start.2 = (f32[1,3,8,64,256]{4,3,2,1,0:T(8,128)S(1)}, f32[1,3,8,64,256]{4,3,2,1,0:T(8,128)}, u32[]{:S(2)}) copy-start(f32[1,3,8,64,256]{4,3,2,1,0:T(8,128)} %param.8) | copy-start | bytes 4718596
  140.4 3.2 %copy-start.18 = (f32[8,64,256]{2,1,0:T(8,128)S(1)}, f32[8,64,256]{2,1,0:T(8,128)}, u32[]{:S(2)}) copy-start(f32[8,64,256]{2,1,0:T(8,128)} %get-tuple-element.32) | copy-start | bytes 1572868
  140.8 2.8 %copy-start.16 = (f32[8,64,256]{2,1,0:T(8,128)S(1)}, f32[8,64,256]{2,1,0:T(8,128)}, u32[]{:S(2)}) copy-start(f32[8,64,256]{2,1,0:T(8,128)} %get-tuple-element.30) | copy-start | bytes 1572868
  140.8 2.8 %copy-start.17 = (f32[8,64,256]{2,1,0:T(8,128)S(1)}, f32[8,64,256]{2,1,0:T(8,128)}, u32[]{:S(2)}) copy-start(f32[8,64,256]{2,1,0:T(8,128)} %get-tuple-element.31) | copy-start | bytes 1572868
  146.7 1.9 %copy-start.8 = (f32[8,64,256]{2,1,0:T(8,128)S(1)}, f32[8,64,256]{2,1,0:T(8,128)}, u32[]{:S(2)}) copy-start(f32[8,64,256]{2,1,0:T(8,128)} %copy-done.7) | copy-start | bytes 1572868
  146.7 1.9 %copy-start.19 = (f32[8,64,2]{2,1,0:T(8,128)S(1)}, f32[8,64,2]{2,1,0:T(8,128)}, u32[]{:S(2)}) copy-start(f32[8,64,2]{2,1,0:T(8,128)} %get-tuple-element.46) | copy-start | bytes 12292
  147.2 4.1 %collective-permute-start.5 = (f32[3,8,64,2]{2,1,3,0:T(8,128)S(1)}, f32[3,8,64,2]{2,1,3,0:T(8,128)S(1)}, u32[]{:S(2)}, u32[]{:S(2)}) collective-permute-start(f32[3,8,64,2]{2,1,3,0:T(8,128)S(1)} %copy.12), channel_id=1, source_target_pairs={{0,128},{1,129},{2,130},{3,131},{4,132},{5,133},{6,134},{7,135},{8... | collective-permute-start | bytes 36872 | tf_op jit(solution)/shard_map/ppermute | solution.py:240
  151.7 1.0 copy-start.9
  151.7 1.2 copy-start.10
  151.7 1.3 copy-start.11
  151.7 1.5 copy-start.12
  151.7 1.6 copy-start.13
  153.4 2.6 %copy-start.4 = (f32[1,8,64,256]{3,2,1,0:T(8,128)S(1)}, f32[1,8,64,256]{3,2,1,0:T(8,128)}, u32[]{:S(2)}) copy-start(f32[1,8,64,256]{3,2,1,0:T(8,128)} %get-tuple-element.26) | copy-start | bytes 1572868
  156.1 4.5 %collective-permute-start.6 = (f32[4,8,2,256]{3,2,1,0:T(2,128)S(1)}, f32[4,8,2,256]{3,2,1,0:T(2,128)S(1)}, u32[]{:S(2)}, u32[]{:S(2)}) collective-permute-start(f32[4,8,2,256]{3,2,1,0:T(2,128)S(1)} %get-tuple-element.20), channel_id=1, source_target_pairs={{32,0},{64,32},{96,64},{0,96},{33,1},{65,33},{97,65},{1,97},{34,2}... | collective-permute-start | bytes 196616 | tf_op jit(solution)/shard_map/ppermute | solution.py:272
  158.7 5.9 %collective-permute-start.7 = (f32[4,8,2,256]{3,2,1,0:T(2,128)S(1)}, f32[4,8,2,256]{3,2,1,0:T(2,128)S(1)}, u32[]{:S(2)}, u32[]{:S(2)}) collective-permute-start(f32[4,8,2,256]{3,2,1,0:T(2,128)S(1)} %get-tuple-element.21), channel_id=1, source_target_pairs={{0,32},{32,64},{64,96},{96,0},{1,33},{33,65},{65,97},{97,1},{2,34}... | collective-permute-start | bytes 196616 | tf_op jit(solution)/shard_map/ppermute | solution.py:270
  166.0 1.0 copy-start.15
  167.1 1.0 copy-start.3
  168.2 12.5 %collective-permute-start.8 = (f32[4,2,64,256]{3,2,1,0:T(8,128)S(1)}, f32[4,2,64,256]{3,2,1,0:T(8,128)S(1)}, u32[]{:S(2)}, u32[]{:S(2)}) collective-permute-start(f32[4,2,64,256]{3,2,1,0:T(8,128)S(1)} %get-tuple-element.14), channel_id=1, source_target_pairs={{1,0},{2,1},{3,2},{4,3},{5,4},{6,5},{7,6},{8,7},{9,8},{10,9},{11,1... | collective-permute-start | bytes 1572872 | tf_op jit(solution)/shard_map/ppermute | solution.py:272
  168.7 12.0 %collective-permute-start.9 = (f32[4,2,64,256]{3,2,1,0:T(8,128)S(1)}, f32[4,2,64,256]{3,2,1,0:T(8,128)S(1)}, u32[]{:S(2)}, u32[]{:S(2)}) collective-permute-start(f32[4,2,64,256]{3,2,1,0:T(8,128)S(1)} %get-tuple-element.15), channel_id=1, source_target_pairs={{0,1},{1,2},{2,3},{3,4},{4,5},{5,6},{6,7},{7,8},{8,9},{9,10},{10,1... | collective-permute-start | bytes 1572872 | tf_op jit(solution)/shard_map/ppermute | solution.py:270
  181.9 1.0 copy-start.14
where the time goes:
time: 189 us; the launch traced here: 185 us
  waiting for transfers between devices  87.3 us (46%)
  starting transfers between devices  47.2 us (25%)
  Pallas kernels  19.9 us (11%)
  other arithmetic  19.9 us (11%)
  local copies, waits for them, and re-layouts  9.66 us (5%)
    all_to_all x2, waiting for transfers between devices, body(): lax.all_to_all(spectrum, axes, split_axis=0, concat_axis=0, tiled=True)  72.7 us
    all_to_all x2, starting transfers between devices, body(): lax.all_to_all(spectrum, axes, split_axis=0, concat_axis=0, tiled=True)  24.2 us
    pallas_call x3, Pallas kernels, call(): pl.pallas_call(kernel, out_shape=jax.ShapeDtypeStruct(shape, F32), in_spe...  19.9 us
    ppermute x2, waiting for transfers between devices, extended_2(): lax.ppermute(head, axis, [((i + 1) % count, i) for i in range(count)])  8.61 us
    ppermute x2, starting transfers between devices, shifted(): lax.ppermute(value, axis, [(source, source + steps) for source in range(i...  7.43 us
    ppermute x2, starting transfers between devices, extended_2(): lax.ppermute(tail, axis, [(i, (i + 1) % count) for i in range(count)])  5.22 us
    unnamed x40, local copies, waits for them, and re-layouts  4.67 us
    ppermute x2, starting transfers between devices, padded(): lax.ppermute(last, axis, up)  4.67 us
  transfers between devices with their start and end apart: 12, of which 6 were waited for; matrix products, arithmetic and copies ran while one was open for 3% of the time, Pallas kernels for 0%

commit v1 on v0

v1 whole, which is shorter than its diff:
```python
import math

import jax
import jax.numpy as jnp
import numpy as np
from jax import lax
from jax.experimental import pallas as pl
from jax.experimental.pallas import tpu as pltpu
from jax.sharding import PartitionSpec as P

TIME_STEP = 0.4
RIM = 3
BF16 = jnp.bfloat16
F32 = jnp.float32


def forward_table(count):
    index = np.arange(count)
    phase = (index[:, None] * index[None, :] % count) * (2.0 * math.pi / count)
    half = count // 2
    alternate = 1.0 - 2.0 * (index % 2)
    table = np.concatenate([np.cos(phase[:half]), alternate[None], -np.sin(phase[1:half])], 0)
    table = table.astype(np.float32)
    high = table.astype(BF16)
    return np.stack([high, (table - high.astype(np.float32)).astype(BF16)])


def split(value):
    high = value.astype(BF16)
    low = (value - high.astype(F32)).astype(BF16)
    return high, low


def turns(product, count):
    phase = (product % count).astype(F32) * (2.0 * math.pi / count)
    return jnp.cos(phase), jnp.sin(phase)


def run_time_tables(start, count, blocks):
    def index(shape, dim):
        return lax.broadcasted_iota(jnp.int32, shape, dim) + start

    shape = (2 * count, 2 * count)
    row, col = index(shape, 0), index(shape, 1)
    local = count // blocks

    def place(i):
        return i % count // 8 * local + i % 4 * 2 + i // count

    def part(i):
        return i // 4 % 2

    cosine, sine = turns((row % count) * place(col), count)
    vertical = jnp.where(
        row // count == part(col), cosine, jnp.where(row < count, sine, -sine)
    )
    cosine, sine = turns((col % count) * place(row), count)
    back = jnp.where(
        col // count == part(row), cosine, jnp.where(col < count, sine, -sine)
    ) * (1.0 / (count * count))
    shape = (count, 2 * count)
    cosine, sine = turns(index(shape, 0) * (index(shape, 1) % count), count)
    lateral = jnp.where(index(shape, 1) < count, cosine, sine)
    shape = (count, count)
    row, col = index(shape, 0), index(shape, 1)
    flip = ((row + col) % count == 0).astype(BF16)
    half = count // 2
    cosine, sine = turns((row % half) * col, count)
    alternate = (1 - 2 * (col % 2)).astype(F32)
    scale = jnp.where(row % half == 0, 1.0, 2.0) * (1.0 / count)
    streamwise = jnp.where(
        row < half, cosine * scale, jnp.where(row == half, alternate * scale, -sine * scale)
    )
    def tripled(table, axis):
        high = lax.reduce_precision(table, 8, 7)
        low = (table - high).astype(BF16)
        high = high.astype(BF16)
        return jnp.concatenate([high, high, low], axis)

    plane = (tripled(vertical, 1), tripled(lateral, 0), tripled(back, 1), flip)
    return plane, tripled(streamwise, 0)


def streamwise_forward(field_any, table_any, out_ref, field_ref, table_ref, sems):
    comps, local_z, local_y, count = field_ref.shape
    rows = local_z * local_y
    half = count // 2
    copies = [pltpu.make_async_copy(table_any, table_ref, sems.at[comps])]
    for c in range(comps):
        copies.append(pltpu.make_async_copy(field_any.at[c], field_ref.at[c], sems.at[c]))
    for copy in copies:
        copy.start()
    copies[0].wait()
    dims = (((1,), (1,)), ((), ()))
    for c in range(comps):
        copies[c + 1].wait()
        high, low = split(field_ref[c].reshape(rows, count))

        def term(i, value):
            return lax.dot_general(table_ref[i], value, dims, preferred_element_type=F32)

        result = term(0, high) + term(0, low) + term(1, high)
        for part in range(2):
            for k in range(0, half, 8):
                for a in range(rows // 128):
                    top = part * half + k
                    out_ref[pl.ds(k * 24 + c * 8 + part * 4 + a, 8, stride=24), :] = result[
                        top : top + 8, a * 128 : (a + 1) * 128
                    ]


def product(left, right):
    return jnp.dot(left, right, preferred_element_type=F32)


def left_product(table, value):
    high, low = split(value)
    return product(table, jnp.concatenate([high, low, high], 0))


def right_product(value, table):
    high, low = split(value)
    return product(jnp.concatenate([high, low, high], 1), table)


def signed_waves(index, count, odd):
    signed = jnp.where(index < count // 2, index, index - count)
    if odd:
        signed = jnp.where(index == count // 2, 0, signed)
    return signed.astype(F32) * (2.0 * math.pi / count)


def plane_kernel(
    owner_ref, in_ref, z_any, y_any, back_any, flip_any, out_ref,
    plain_ref, z_ref, y_ref, back_ref, flip_ref, sems,
):
    n = y_ref.shape[1] // 2
    pairs = ((z_any, z_ref), (y_any, y_ref), (back_any, back_ref), (flip_any, flip_ref))
    copies = [pltpu.make_async_copy(s, d, sems.at[i]) for i, (s, d) in enumerate(pairs)]
    for copy in copies:
        copy.start()
    owner = owner_ref[0]
    is_packed = owner == 0
    low_lanes = lax.broadcasted_iota(jnp.int32, (n, 128), 1) < 64
    row = lax.broadcasted_iota(jnp.int32, (n, n), 0)
    col = lax.broadcasted_iota(jnp.int32, (n, n), 1)
    wave_x = owner.astype(F32) * (2.0 * math.pi / n)
    wave_z = signed_waves(row, n, False)
    wave_y = signed_waves(col, n, False)
    curl_z = signed_waves(row, n, True)
    curl_y = signed_waves(col, n, True)
    plane = wave_y * wave_y + wave_z * wave_z
    squared = plane + wave_x * wave_x
    scale = jnp.where(squared > 0, 1.0 / jnp.where(squared > 0, squared, 1.0), 0.0)
    top_scale = 1.0 / (plane + math.pi * math.pi)
    sigma = jnp.where(is_packed, 0.5 * (scale + top_scale), scale)
    delta = 0.5 * (scale - top_scale)
    copies[0].wait()
    copies[1].wait()
    copies[3].wait()
    for c in range(3):
        blocks = [
            in_ref[32 * g : 32 * g + 32, 8 * c : 8 * c + 8, :].reshape(n, 128) for g in range(4)
        ]
        tops, bottoms = [], []
        for g in (0, 2):
            first, second = blocks[g], blocks[g + 1]
            tops.append(jnp.where(low_lanes, first, pltpu.roll(second, 64, 1)))
            bottoms.append(jnp.where(low_lanes, pltpu.roll(first, 64, 1), second))
        value = jnp.concatenate(
            [jnp.concatenate(tops, 1), jnp.concatenate(bottoms, 1)], 0
        )
        value = left_product(z_ref[...], value)
        value = right_product(value, y_ref[...])
        real_cos, real_sin = value[:n, :n], value[:n, n:]
        imag_cos, imag_sin = value[n:, :n], value[n:, n:]
        plain_ref[c, :n, :] = (real_cos + imag_sin) * sigma
        plain_ref[c, n:, :] = (imag_cos - real_sin) * sigma

        @pl.when(is_packed)
        def _():
            turned = jnp.concatenate([real_cos - imag_sin, imag_cos + real_sin], 1)
            high, low = split(turned)
            mirror = product(flip_ref[...], high) + product(flip_ref[...], low)
            plain_ref[c, :n, :] += mirror[:, :n] * delta
            plain_ref[c, n:, :] -= mirror[:, n:] * delta

    copies[2].wait()
    for c in range(3):
        if c == 0:
            def cross(part):
                return curl_y * plain_ref[2, part] - curl_z * plain_ref[1, part]
        elif c == 1:
            def cross(part):
                return curl_z * plain_ref[0, part] - wave_x * plain_ref[2, part]
        else:
            def cross(part):
                return wave_x * plain_ref[1, part] - curl_y * plain_ref[0, part]
        value = jnp.concatenate([-cross(slice(n, 2 * n)), cross(slice(0, n))], 0)
        value = right_product(value, y_ref[...])
        real = value[:n, :n] - value[n:, n:]
        imag = value[n:, :n] + value[:n, n:]
        value = left_product(back_ref[...], jnp.concatenate([real, imag], 0))
        for pair in range(2):
            top = value[:n, 128 * pair : 128 * pair + 128]
            bottom = value[n:, 128 * pair : 128 * pair + 128]
            first = jnp.where(low_lanes, top, pltpu.roll(bottom, 64, 1))
            second = jnp.where(low_lanes, pltpu.roll(top, 64, 1), bottom)
            for g, block in ((2 * pair, first), (2 * pair + 1, second)):
                out_ref[32 * g : 32 * g + 32, 8 * c : 8 * c + 8, :] = block.reshape(32, 8, 128)


def streamwise_backward(
    in_ref, table_ref, drift_ref, out_ref, speed_ref, low_ref, high_ref
):
    comps, local_z, local_y, count = out_ref.shape

    def component(c, carry):
        parts = []
        for part in range(2):
            chunks = [
                in_ref[pl.ds(c * 8 + part * 4 + a, count // 2, stride=24), :] for a in range(4)
            ]
            parts.append(jnp.concatenate(chunks, 1))
        value = jnp.concatenate(parts, 0).T
        result = right_product(value, table_ref[...]) + drift_ref[0, c]
        out_ref[c] = result.reshape(local_z, local_y, count)
        speed_ref[c] = result.reshape(local_z, local_y, count)
        return carry

    lax.fori_loop(0, comps, component, 0)
    for c in range(comps):
        for z in range(local_z):
            row = (c * local_z + z) * RIM
            low_ref[row : row + RIM, :] = out_ref[c, z, 0:RIM, :]
            high_ref[row : row + RIM, :] = out_ref[c, z, local_y - RIM : local_y, :]


def edge_kernel(speed_ref, above_ref, below_ref, tail_ref, up_ref, down_ref):
    comps, local_z, local_y, count = speed_ref.shape
    for c in range(comps):
        for z in range(local_z):
            row = (c * local_z + z) * RIM
            tail_ref[c, z, 0:RIM, :] = above_ref[row : row + RIM, :]
            tail_ref[c, z, RIM : 8 - RIM, :] = jnp.zeros((8 - 2 * RIM, count), F32)
            tail_ref[c, z, 8 - RIM : 8, :] = below_ref[row : row + RIM, :]
        for target, first in ((up_ref, local_z - RIM), (down_ref, 0)):
            for z in range(RIM):
                target[c, z, 0:local_y, :] = speed_ref[c, first + z]
                target[c, z, local_y : local_y + 8, :] = tail_ref[c, first + z]


def weights(shift, small=False):
    zero = jnp.zeros_like(shift)
    if small:
        left = shift < 0
        frac = jnp.where(left, shift + 1.0, shift)
    else:
        base = jnp.floor(shift)
        frac = shift - base
    rest = 1.0 - frac
    side = -0.5 * frac * rest
    before = side * rest
    after = side * frac
    near = 1.0 + frac * frac * (1.5 * frac - 2.5)
    far = 1.0 - (before + near + after)
    if small:
        values = [zero, before, near, far, after, zero]
        return {o: jnp.where(left, values[o + 3], values[o + 2]) for o in range(-2, 3)}
    at = {k: base == k for k in range(-4, 4)}
    result = {}
    for o in range(-2, 3):
        value = jnp.where(at[o - 2], after, zero)
        value = jnp.where(at[o - 1], far, value)
        value = jnp.where(at[o], near, value)
        result[o] = jnp.where(at[o + 1], before, value)
    return result


def rotated(value, steps):
    return pltpu.roll(value, steps % value.shape[1], 1)


def inflow_kernel(wake_ref, speed_ref, tail_ref, low_ref, high_ref, field_ref, out_ref, line_ref):
    planes, local_z = field_ref.shape[1], speed_ref.shape[1]
    lane = lax.broadcasted_iota(jnp.int32, (72, 128), 1)

    @pl.when(wake_ref[0] == 0)
    def _():
        line_ref[...] = jnp.zeros(line_ref.shape, F32)
        for q in range(planes + 2):
            columns = jnp.zeros((72, 128), F32)
            for c in range(3):
                if q < RIM:
                    first, last = low_ref[c, q, :, :128], low_ref[c, q, :, 128:]
                elif q < RIM + local_z:
                    z = q - RIM
                    pieces = [
                        jnp.concatenate([speed_ref[c, z, :, lanes], tail_ref[c, z, :, lanes]], 0)
                        for lanes in (slice(0, 128), slice(128, 256))
                    ]
                    first, last = pieces
                else:
                    z = q - RIM - local_z
                    first, last = high_ref[c, z, :, :128], high_ref[c, z, :, 128:]
                at = 4 * c
                here = (lane >= at) & (lane < at + 3)
                columns = jnp.where(here, rotated(last, at + 3), columns)
                columns = jnp.where(lane == at + 3, rotated(first, at + 3), columns)
                if 1 <= q <= planes:
                    at = 12 + 2 * c
                    here = (lane >= at) & (lane < at + 2)
                    columns = jnp.where(
                        here, rotated(field_ref[c, q - 1, :, 128:], at + 2), columns
                    )
            gap = jnp.zeros((40, 128), F32)
            whole = jnp.concatenate([columns, columns[:8], gap, columns[64:]], 0)
            line_ref[24 * q : 24 * q + 24, :] = whole.T[:24]

        def line(row, plane):
            return line_ref[pl.ds(24 * plane + row, 16, stride=24), :]

        shift = [weights(TIME_STEP * line(x, 1)) for x in (1, 2)]
        part = [[line(12 + 2 * c + x, 1) for x in range(2)] for c in range(3)]
        for c in range(3):
            strength = []
            for x in range(2):
                row = 4 * c + 1 + x
                value = line(row, 1)
                strength.append(
                    part[c][x]
                    + (0.5 * TIME_STEP)
                    * (
                        part[0][x] * (line(row + 1, 1) - line(row - 1, 1))
                        + part[1][x] * (rotated(value, -1) - rotated(value, 1))
                        + part[2][x] * (line(row, 2) - line(row, 0))
                    )
                )
            rows = (
                strength[0] * shift[0][2] + strength[1] * shift[1][1],
                strength[1] * shift[1][2],
                line(4 * c + 2, 1),
            )
            for i, row in enumerate(rows):
                out_ref[pl.ds(4 * c + i, 16, stride=16), :] = row


def fill_speed(speed_ref, tail_ref, low_ref, high_ref, all_ref):
    local_z = speed_ref.shape[1]
    most = jnp.zeros((8, 128), F32)
    for c in range(3):
        for t in range(2):
            lanes = slice(128 * t, 128 * t + 128)
            for own, end, row, first in (
                (low_ref, low_ref, 64, 0),
                (speed_ref, tail_ref, 0, RIM),
                (high_ref, high_ref, 64, RIM + local_z),
            ):
                planes = slice(first, first + own.shape[1])
                body = own[c, :, 0:64, lanes]
                tail = end[c, :, row : row + 8, lanes]
                all_ref[c, planes, t, 8:72, :] = body
                all_ref[c, planes, t, 0:8, :] = tail
                all_ref[c, planes, t, 72:80, :] = tail
                all_ref[c, planes, t, 80:88, :] = body[:, 0:8]
                most = jnp.maximum(most, jnp.max(jnp.abs(body).reshape(-1, 8, 128), 0))
                most = jnp.maximum(most, jnp.max(jnp.abs(tail), 0))
    return jnp.max(most)


def wake_kernel(
    wake_ref, speed_ref, tail_ref, low_ref, high_ref, field_ref, inflow_ref, out_ref,
    all_ref, column_ref, moved_ref, across_ref, lateral_ref, upward_ref,
):
    planes = field_ref.shape[1]
    local_z, local_y = out_ref.shape[1], out_ref.shape[2]
    size = 72
    lane = lax.broadcasted_iota(jnp.int32, (size, 128), 1)
    is_wake = wake_ref[0] != 0
    entering_lane = is_wake & (lane == 0)
    leaving_lane = is_wake & (lane == 127)
    crossing = {o: is_wake & (lane >= 128 - o if o > 0 else lane < -o) for o in (-2, -1, 1, 2)}
    most = fill_speed(speed_ref, tail_ref, low_ref, high_ref, all_ref)
    is_small = TIME_STEP * most < 0.999

    def turned(pair, o):
        first, second = rotated(pair[0], o), rotated(pair[1], o)
        swap = lane < o if o > 0 else lane >= 128 + o
        return jnp.where(swap, second, first), jnp.where(swap, first, second)

    def step(p, small):
        column_ref[...] = jnp.concatenate(
            [inflow_ref[pl.ds(16 * p, 16), :], jnp.zeros((112, 128), F32)], 0
        ).T
        for block in range(72 // size):
            here = slice(size * block, size * block + size)
            kept = slice(8 + size * block, 8 + size * block + size)
            is_end = block == 72 // size - 1

            def velocity(c, plane, t, steps=0):
                row = 8 + size * block + steps
                return all_ref[c, plane, t, row : row + size, :]

            inflow = column_ref[here, :]
            along = []
            for t in range(2):
                along.append(weights(TIME_STEP * velocity(0, p + 1, t), small))
                across = weights(TIME_STEP * velocity(1, p + 1, t), small)
                for o in range(-2, 3):
                    across_ref[o + 2, t, kept, :] = across[o]
                    if is_end:
                        across_ref[o + 2, t, 0:8, :] = across[o][size - 8 :]
            for o in (-2, -1, 1, 2):
                t = 1 if o > 0 else 0
                along[t][o] = jnp.where(crossing[o], 0.0, along[t][o])
            part = [
                [field_ref[c, p, here, 128 * t : 128 * t + 128] for t in range(2)]
                for c in range(3)
            ]
            for c in range(3):
                value = [velocity(c, p + 1, t) for t in range(2)]
                ahead, behind = list(turned(value, -1)), list(turned(value, 1))
                behind[0] = jnp.where(entering_lane, rotated(inflow, -(4 * c + 2)), behind[0])
                ahead[1] = jnp.where(leaving_lane, value[1], ahead[1])
                strength = []
                for t in range(2):
                    strength.append(
                        part[c][t]
                        + (0.5 * TIME_STEP)
                        * (
                            part[0][t] * (ahead[t] - behind[t])
                            + part[1][t] * (velocity(c, p + 1, t, 1) - velocity(c, p + 1, t, -1))
                            + part[2][t] * (velocity(c, p + 2, t) - velocity(c, p, t))
                        )
                    )
                total = [strength[t] * along[t][0] for t in range(2)]
                total[0] = total[0] + jnp.where(lane < 2, rotated(inflow, -4 * c), 0.0)
                for o in (-2, -1, 1, 2):
                    pair = turned([strength[t] * along[t][o] for t in range(2)], o)
                    total = [total[t] + pair[t] for t in range(2)]
                for t in range(2):
                    moved_ref[c, t, kept, :] = total[t]
                    if is_end:
                        moved_ref[c, t, 0:8, :] = total[t][size - 8 :]
        tall = 32
        for block in range(local_y // tall):
            here = slice(tall * block, tall * block + tall)
            for t in range(2):
                total = [jnp.zeros((tall, 128), F32) for _ in range(3)]
                for o in range(-2, 3):
                    first = 8 + tall * block - o
                    weight = across_ref[o + 2, t, first : first + tall, :]
                    for c in range(3):
                        term = moved_ref[c, t, first : first + tall, :] * weight
                        total[c] = term if o == -2 else total[c] + term
                for c in range(3):
                    lateral_ref[c, p, t, here, :] = total[c]
                first = 8 + tall * block
                upward = weights(
                    TIME_STEP * all_ref[2, p + 1, t, first : first + tall, :], small
                )
                for o in range(-2, 3):
                    upward_ref[o + 2, p, t, here, :] = upward[o]

    def run(small):
        def one(p, carry):
            step(p, small)
            return carry

        lax.fori_loop(0, planes, one, 0)

    @pl.when(is_small)
    def _():
        run(True)

    @pl.when(jnp.logical_not(is_small))
    def _():
        run(False)

    def gather(z, carry):
        tall = 32
        for t in range(2):
            for block in range(local_y // tall):
                here = slice(tall * block, tall * block + tall)
                total = [None] * 3
                for o in range(-2, 3):
                    weight = upward_ref[o + 2, z + 2 - o, t, here, :]
                    for c in range(3):
                        term = lateral_ref[c, z + 2 - o, t, here, :] * weight
                        total[c] = term if o == -2 else total[c] + term
                for c in range(3):
                    out_ref[c, z, here, 128 * t : 128 * t + 128] = total[c]
        return carry

    lax.fori_loop(0, local_z, gather, 0)


def call(kernel, shapes, args, smem=(), far=(), scratch=(), limit=24):
    single = not isinstance(shapes, list)
    outs = [jax.ShapeDtypeStruct(s, F32) for s in ([shapes] if single else shapes)]
    def space(i):
        return pltpu.SMEM if i in smem else pltpu.HBM if i in far else pltpu.VMEM

    specs = [pl.BlockSpec(memory_space=space(i)) for i in range(len(args))]
    out = pl.pallas_call(
        kernel,
        out_shape=outs,
        in_specs=specs,
        out_specs=[pl.BlockSpec(memory_space=pltpu.VMEM) for _ in outs],
        scratch_shapes=list(scratch),
        compiler_params=pltpu.CompilerParams(vmem_limit_bytes=limit * 1024 * 1024),
    )(*args)
    return out[0] if single else out


def forward_lines(field):
    count = field.shape[3]
    table = jnp.asarray(forward_table(count))
    scratch = (
        pltpu.VMEM(field.shape, F32),
        pltpu.VMEM(table.shape, BF16),
        pltpu.SemaphoreType.DMA((field.shape[0] + 1,)),
    )
    shape = (count // 2 * 24, 128)
    return call(streamwise_forward, shape, (field, table), far=(0, 1), scratch=scratch, limit=61)


def solve_plane(spectrum, owner, tables):
    count = tables[3].shape[1]
    args = (owner.reshape(1), spectrum, *tables)
    scratch = [pltpu.VMEM((3, 2 * count, count), F32)]
    scratch += [pltpu.VMEM(t.shape, t.dtype) for t in tables]
    scratch += [pltpu.SemaphoreType.DMA((len(tables),))]
    far = (2, 3, 4, 5)
    return call(
        plane_kernel, spectrum.shape, args, smem=(0,), far=far, scratch=scratch, limit=54
    )


def backward_lines(spectrum, drift, table, shape):
    edge = (shape[0] * shape[1] * RIM, shape[3])
    shapes = [shape, shape, edge, edge]
    return call(streamwise_backward, shapes, (spectrum, table, drift), smem=(2,))


def with_edges(speed, above, below):
    comps, local_z, local_y, count = speed.shape
    send = (comps, RIM, local_y + 8, count)
    shapes = [(comps, local_z, 8, count), send, send]
    return call(edge_kernel, shapes, (speed, above, below))


def inflow_columns(wake, speed, tail, low, high, field):
    args = (wake, speed, tail, low, high, field)
    scratch = [pltpu.VMEM((24 * (field.shape[1] + 6), 128), F32)]
    return call(inflow_kernel, (256, 128), args, smem=(0,), scratch=scratch)


def wake_step(wake, speed, tail, low, high, field, inflow):
    comps, local_z, local_y, count = speed.shape
    lanes, planes = count // 128, local_z + 4
    scratch = [
        pltpu.VMEM((comps, planes + 2, lanes, local_y + 24, 128), F32),
        pltpu.VMEM((128, 128), F32),
        pltpu.VMEM((comps, lanes, local_y + 16, 128), F32),
        pltpu.VMEM((5, lanes, local_y + 16, 128), F32),
        pltpu.VMEM((comps, planes, lanes, local_y, 128), F32),
        pltpu.VMEM((5, planes, lanes, local_y, 128), F32),
    ]
    args = (wake, speed, tail, low, high, field, inflow)
    return call(wake_kernel, speed.shape, args, smem=(0,), scratch=scratch)


def from_before(value, axis):
    count = lax.axis_size(axis)
    return lax.ppermute(value, axis, [(i, (i + 1) % count) for i in range(count)])


def from_after(value, axis):
    count = lax.axis_size(axis)
    return lax.ppermute(value, axis, [((i + 1) % count, i) for i in range(count)])


def wider_rows(field):
    above = from_after(field[:, :, :2], "gy")
    below = from_before(field[:, :, field.shape[2] - 2 :], "gy")
    above = jnp.pad(above, ((0, 0), (0, 0), (0, 4), (0, 0)))
    return jnp.concatenate([field, above, below], 2)


def wider_planes(field):
    low = from_before(field[:, field.shape[1] - 2 :], "gz")
    high = from_after(field[:, :2], "gz")
    return jnp.concatenate([low, field, high], 1)


def body(vorticity, wind):
    wake = (lax.axis_index("grp") == 1).astype(jnp.int32).reshape(1)
    field = vorticity[0]
    count_x = field.shape[3]
    size_gz = lax.axis_size("gz")
    groups = lax.axis_size("gy") * size_gz
    owner = lax.axis_index("gy") * size_gz + lax.axis_index("gz")
    axes = ("gy", "gz")
    spectrum = forward_lines(field)
    start = lax.axis_index("grp") * 0
    spectrum, start, halo_field = lax.optimization_barrier((spectrum, start, field))
    spectrum = spectrum.reshape(groups, 24, 128)
    spectrum = lax.all_to_all(spectrum, axes, split_axis=0, concat_axis=0, tiled=True)
    wide = wider_rows(halo_field)
    tables, streamwise = run_time_tables(start, count_x, size_gz)
    spectrum, wide, tables, streamwise = lax.optimization_barrier(
        (spectrum, wide, tables, streamwise)
    )
    spectrum = solve_plane(spectrum, owner, tables)
    spectrum, wide = lax.optimization_barrier((spectrum, wide))
    spectrum = lax.all_to_all(spectrum, axes, split_axis=0, concat_axis=0, tiled=True)
    wide = wider_planes(wide)
    spectrum, wide = lax.optimization_barrier((spectrum, wide))
    spectrum = spectrum.reshape(groups * 24, 128)
    velocity, speed, first, last = backward_lines(spectrum, wind, streamwise, field.shape)
    above, below = from_after(first, "gy"), from_before(last, "gy")
    tail, up, down = with_edges(speed, above, below)
    low, high = from_before(up, "gz"), from_after(down, "gz")
    inflow = inflow_columns(wake, speed, tail, low, high, wide)
    inflow = lax.ppermute(inflow, "grp", [(0, 1)])
    result = wake_step(wake, speed, tail, low, high, wide, inflow)
    return (result[None], velocity[None])


def solution(mesh):
    return jax.shard_map(
        body,
        mesh=mesh,
        in_specs=(P("grp", None, "gz", "gy", None), P("grp", None)),
        out_specs=(P("grp", None, "gz", "gy", None), P("grp", None, "gz", "gy", None)),
        check_vma=False,
    )
```

time: 189 us -> 175 us (0.926); the launches traced: 185 us -> 175 us
  waiting for transfers between devices: 87.3 us -> 66.4 us
  Pallas kernels: 19.9 us -> 39 us
  local copies, waits for them, and re-layouts: 9.66 us -> 3.68 us
  starting transfers between devices: 47.2 us -> 43.1 us
  other arithmetic: 19.9 us -> 21.8 us
    all_to_all x2, waiting for transfers between devices: 72.7 us -> 23.1 us  [body(): lax.all_to_all(spectrum, axes, split_axis=0, concat_axis=0, tiled=True)]
    ppermute x10 -> x9, waiting for transfers between devices: 14.6 us -> 43.4 us  [the longest x4 30.5 us: from_before(): lax.ppermute(value, axis, [(i, (i + 1) % count) for i in range(count)])]
    pallas_call x3 -> x6, Pallas kernels: 19.9 us -> 39 us  [call(): pl.pallas_call(kernel, out_shape=outs, in_specs=specs, out_specs=[pl.Bloc...]
    convert_element_type x0 -> x4, other arithmetic: none -> 14.9 us  [the longest x3 14 us: tripled(): high = high.astype(BF16)]
    add x3, other arithmetic: 6.62 us -> 0.03 us  [the longest x1 0.01 us: index(): return lax.broadcasted_iota(jnp.int32, shape, dim) + start]
    mul x4 -> x0, other arithmetic: 5.78 us -> none  [the longest x2 3.11 us: body(): rim_cols[:3, start:start + width_z, :, :]]
    ppermute x10 -> x9, starting transfers between devices: 23 us -> 17.2 us  [the longest x4 9.6 us: from_before(): lax.ppermute(value, axis, [(i, (i + 1) % count) for i in range(count)])]
    concatenate x2 -> x6, other arithmetic: 1.11 us -> 6.82 us  [the longest x4 3.51 us: tripled(): return jnp.concatenate([high, high, low], axis)]
  transfers between devices with their start and end apart: 12 -> 11, of which waited for: 6 -> 10; matrix products, arithmetic and copies ran while one was open for 3% -> 13% of each run, Pallas kernels for 0% -> 0%
where the time goes in v1:
time: 175 us
  waiting for transfers between devices  66.4 us (38%)
  starting transfers between devices  43.1 us (25%)
  Pallas kernels  39 us (22%)
  other arithmetic  21.8 us (12%)
  local copies, waits for them, and re-layouts  3.68 us (2%)
    pallas_call x6, Pallas kernels, call(): pl.pallas_call(kernel, out_shape=outs, in_specs=specs, out_specs=[pl.Bloc...  39 us
    ppermute x4, waiting for transfers between devices, from_before(): lax.ppermute(value, axis, [(i, (i + 1) % count) for i in range(count)])  30.5 us
    all_to_all x2, starting transfers between devices, body(): lax.all_to_all(spectrum, axes, split_axis=0, concat_axis=0, tiled=True)  25.9 us
    all_to_all x2, waiting for transfers between devices, body(): lax.all_to_all(spectrum, axes, split_axis=0, concat_axis=0, tiled=True)  23.1 us
    convert_element_type x3, other arithmetic, tripled(): high = high.astype(BF16)  14 us
    ppermute x4, waiting for transfers between devices, from_after(): lax.ppermute(value, axis, [((i + 1) % count, i) for i in range(count)])  11 us
    ppermute x4, starting transfers between devices, from_before(): lax.ppermute(value, axis, [(i, (i + 1) % count) for i in range(count)])  9.6 us
    ppermute x1, starting transfers between devices, body(): inflow = lax.ppermute(inflow, 'grp', [(0, 1)])  4.45 us
  transfers between devices with their start and end apart: 11, of which 10 were waited for; matrix products, arithmetic and copies ran while one was open for 13% of the time, Pallas kernels for 0%

profile of v1, /device:TPU:31, one launch (start us, length us, event | category | flops | bytes accessed | tf_op | source)
XLA Modules:
  0.0 174.9 jit_solution(11485900153165020860)
XLA Ops:
  0.6 3.6 %shard_map.50 = f32[3072,128]{1,0:T(8,128)} custom-call(f32[3,8,64,256]{3,2,1,0:T(8,128)} %bitcast.7, bf16[2,256,256]{2,1,0:T(8,128)(2,1)} %constant.213.clone.table_any), custom_call_target="tpu_custom_call" | custom-call | tf_op jit(solution)/shard_map/pallas_call | solution.py:505
  4.3 13.3 %all-to-all-start = ((f32[128,24,128]{2,1,0:T(8,128)}), f32[128,24,128]{2,1,0:T(8,128)}, u32[]{:S(2)}, u32[]{:S(2)}) async-start(f32[128,24,128]{2,1,0:T(8,128)} %bitcast.10), calls=%async_computation | async-start | bytes 3145728 | tf_op jit(solution)/shard_map/all_to_all | solution.py:609
  17.5 1.1 fusion.49
  18.6 1.5 collective-permute-start.1
  20.1 2.5 %collective-permute-start = (f32[3,8,2,256]{3,2,1,0:T(2,128)S(1)}, f32[3,8,2,256]{3,2,1,0:T(2,128)S(1)}, u32[]{:S(2)}, u32[]{:S(2)}) collective-permute-start(f32[3,8,2,256]{3,2,1,0:T(2,128)S(1)} %get-tuple-element.47), channel_id=1, source_target_pairs={{32,0},{64,32},{96,64},{0,96},{33,1},{65,33},{97,65},{1,97},{34,2}... | collective-permute-start | bytes 147464 | tf_op jit(solution)/shard_map/ppermute | solution.py:581
  22.7 2.5 %reduce-precision_convert_fusion.2 = (bf16[256,512]{1,0:T(8,128)(2,1)S(1)}, bf16[256,512]{1,0:T(8,128)(2,1)S(1)}) fusion(s32[512]{0:T(512)S(1)} %get-tuple-element.59, s32[512]{0:T(512)S(1)} %get-tuple-element.73, pred[512]{0:T(512)(128)(4,1)S(1)} %get-tuple-element.64, s32[256]{0:T(256)S(1)} %get-tuple-element.68, pred[512]{0:T(512)(128)(4,1)S(1)} %get-tuple-element.60), kind=kLoop, calls=%fused_computation.82 | loop fusion | flops 2621440 | bytes 530432 | tf_op jit(solution)/shard_map/convert_element_type | solution.py:77
  25.3 1.0 pad_maximum_fusion.3.y_any
  26.3 0.8 fusion.40.flip_any
  27.1 1.5 reduce-precision_convert_fusion.3
  28.6 10.0 %reduce-precision_convert_fusion = (bf16[512,512]{1,0:T(8,128)(2,1)S(1)}, bf16[512,512]{1,0:T(8,128)(2,1)S(1)}, bf16[512,512]{1,0:T(8,128)(2,1)S(1)}, bf16[512,512]{1,0:T(8,128)(2,1)S(1)}) fusion(pred[512]{0:T(512)(128)(4,1)S(1)} %get-tuple-element.60, s32[512]{0:T(512)S(1)} %get-tuple-element.58, s32[512]{0:T(512)S(1)} %get-tuple-element.75, ...), kind=kLoop, calls=%fused_computation.43 | loop fusion | flops 29622272 | bytes 2116096 | tf_op jit(solution)/shard_map/convert_element_type | solution.py:77
  38.6 1.3 pad_maximum_fusion.2.back_any
  39.9 1.2 pad_maximum_fusion.1.z_any
  41.1 6.1 %collective-permute-done.1 = f32[3,8,2,256]{3,2,1,0:T(2,128)S(1)} collective-permute-done((f32[3,8,2,256]{3,2,1,0:T(2,128)S(1)}, f32[3,8,2,256]{3,2,1,0:T(2,128)S(1)}, u32[]{:S(2)}, u32[]{:S(2)}) %collective-permute-start.1) | collective-permute-done | bytes 49184 | tf_op jit(solution)/shard_map/ppermute | solution.py:576
  47.2 0.0 collective-permute-done
  47.2 1.6 fusion
  48.8 0.0 copy-start.3
  48.8 6.6 %all-to-all-done.in_ref = f32[128,24,128]{2,1,0:T(8,128)} async-done(((f32[128,24,128]{2,1,0:T(8,128)}), f32[128,24,128]{2,1,0:T(8,128)}, u32[]{:S(2)}, u32[]{:S(2)}) %all-to-all-start) | async-done | bytes 1572896 | tf_op jit(solution)/shard_map/all_to_all | solution.py:609
  55.4 14.1 %shard_map.51 = f32[128,24,128]{2,1,0:T(8,128)} custom-call(s32[1]{0:T(128)} %bitcast.1.owner_ref, f32[128,24,128]{2,1,0:T(8,128)} %all-to-all-done.in_ref, bf16[512,1536]{1,0:T(8,128)(2,1)} %pad_maximum_fusion.1.z_any, bf16[768,512]{1,0:T(8,128)(2,1)} %pad_maximum_fusion.3.y_any, bf16[512,1536]{1,0:T(8,128)(2,1)} %pad_maximum_fusion.2.back_any, ...), custom_call_target="tpu_custom_call" | custom-call | tf_op jit(solution)/shard_map/pallas_call | solution.py:505
  69.5 12.7 %all-to-all-start.1 = ((f32[128,24,128]{2,1,0:T(8,128)}), f32[128,24,128]{2,1,0:T(8,128)}, u32[]{:S(2)}, u32[]{:S(2)}) async-start(f32[128,24,128]{2,1,0:T(8,128)} %shard_map.51), calls=%async_computation.1 | async-start | bytes 3145728 | tf_op jit(solution)/shard_map/all_to_all | solution.py:617
  82.2 0.0 copy-done.3
  82.2 0.1 fusion.48
  82.2 0.9 collective-permute-start.2
  83.2 0.0 copy-start.2
  83.2 0.0 collective-permute-start.3
  83.2 14.0 %collective-permute-done.2 = f32[3,2,72,256]{3,2,1,0:T(8,128)S(1)} collective-permute-done((f32[3,2,72,256]{3,2,1,0:T(8,128)S(1)}, f32[3,2,72,256]{3,2,1,0:T(8,128)S(1)}, u32[]{:S(2)}, u32[]{:S(2)}) %collective-permute-start.2) | collective-permute-done | bytes 442400 | tf_op jit(solution)/shard_map/ppermute | solution.py:576
  97.2 3.4 %collective-permute-done.3 = f32[3,2,72,256]{3,2,1,0:T(8,128)S(1)} collective-permute-done((f32[3,2,72,256]{3,2,1,0:T(8,128)S(1)}, f32[3,2,72,256]{3,2,1,0:T(8,128)S(1)}, u32[]{:S(2)}, u32[]{:S(2)}) %collective-permute-start.3) | collective-permute-done | bytes 442400 | tf_op jit(solution)/shard_map/ppermute | solution.py:581
  100.7 1.7 pad_maximum_fusion.field_ref
  102.4 16.5 %all-to-all-done.1 = f32[128,24,128]{2,1,0:T(8,128)} async-done(((f32[128,24,128]{2,1,0:T(8,128)}), f32[128,24,128]{2,1,0:T(8,128)}, u32[]{:S(2)}, u32[]{:S(2)}) %all-to-all-start.1) | async-done | bytes 1572896 | tf_op jit(solution)/shard_map/all_to_all | solution.py:617
  118.9 0.0 copy-done.2
  118.9 3.8 %shard_map.52 = (f32[3,8,64,256]{3,2,1,0:T(8,128)}, f32[3,8,64,256]{3,2,1,0:T(8,128)S(1)}, f32[72,256]{1,0:T(8,128)S(1)}, f32[72,256]{1,0:T(8,128)S(1)}) custom-call(f32[3072,128]{1,0:T(8,128)} %bitcast.4.in_ref, bf16[768,256]{1,0:T(8,128)(2,1)S(1)} %pad_maximum_fusion.4.table_ref, f32[1,3]{1,0:T(1,128)S(1)} %copy-done.2), custom_call_target="tpu_custom_call" | custom-call | tf_op jit(solution)/shard_map/pallas_call | solution.py:505
  122.7 0.7 collective-permute-start.4
  123.3 0.8 collective-permute-start.5
  124.2 1.7 collective-permute-done.4.above_ref
  125.9 2.5 %collective-permute-done.5.below_ref = f32[72,256]{1,0:T(8,128)S(1)} collective-permute-done((f32[72,256]{1,0:T(8,128)S(1)}, f32[72,256]{1,0:T(8,128)S(1)}, u32[]{:S(2)}, u32[]{:S(2)}) %collective-permute-start.5) | collective-permute-done | bytes 73760 | tf_op jit(solution)/shard_map/ppermute | solution.py:576
  128.3 1.2 shard_map.53
  129.6 0.0 copy-start
  129.6 1.1 copy-done
  130.7 6.4 %collective-permute-start.6 = (f32[3,3,72,256]{3,2,1,0:T(8,128)}, f32[3,3,72,256]{3,2,1,0:T(8,128)S(1)}, u32[]{:S(2)}, u32[]{:S(2)}) collective-permute-start(f32[3,3,72,256]{3,2,1,0:T(8,128)} %get-tuple-element.40), channel_id=1, source_target_pairs={{0,1},{1,2},{2,3},{3,4},{4,5},{5,6},{6,7},{7,8},{8,9},{9,10},{10,1... | collective-permute-start | bytes 1990664 | tf_op jit(solution)/shard_map/ppermute | solution.py:576
  137.1 0.0 collective-permute-start.7
  137.1 7.9 %collective-permute-done.6.low_ref = f32[3,3,72,256]{3,2,1,0:T(8,128)S(1)} collective-permute-done((f32[3,3,72,256]{3,2,1,0:T(8,128)}, f32[3,3,72,256]{3,2,1,0:T(8,128)S(1)}, u32[]{:S(2)}, u32[]{:S(2)}) %collective-permute-start.6) | collective-permute-done | bytes 663584 | tf_op jit(solution)/shard_map/ppermute | solution.py:576
  145.0 5.8 %collective-permute-done.7.high_ref = f32[3,3,72,256]{3,2,1,0:T(8,128)} collective-permute-done((f32[3,3,72,256]{3,2,1,0:T(8,128)}, f32[3,3,72,256]{3,2,1,0:T(8,128)}, u32[]{:S(2)}, u32[]{:S(2)}) %collective-permute-start.7) | collective-permute-done | bytes 663584 | tf_op jit(solution)/shard_map/ppermute | solution.py:581
  150.8 0.0 copy-start.1
  150.8 1.4 copy-done.1
  152.2 2.7 %shard_map.54 = f32[256,128]{1,0:T(8,128)S(1)} custom-call(s32[1]{0:T(128)} %bitcast.wake_ref, f32[3,8,64,256]{3,2,1,0:T(8,128)S(1)} %copy-done.1, f32[3,8,8,256]{3,2,1,0:T(8,128)S(1)} %get-tuple-element.39.tail_ref, f32[3,3,72,256]{3,2,1,0:T(8,128)S(1)} %collective-permute-done.6.low_ref, f32[3,3,72,256]{3,2,1,0:T(8,128)} %collective-permute-done.7.high_ref, ...), custom_call_target="tpu_custom_call" | custom-call | tf_op jit(solution)/shard_map/pallas_call | solution.py:505
  155.0 4.5 %collective-permute-start.8 = (f32[256,128]{1,0:T(8,128)S(1)}, f32[256,128]{1,0:T(8,128)S(1)}, u32[]{:S(2)}, u32[]{:S(2)}) collective-permute-start(f32[256,128]{1,0:T(8,128)S(1)} %shard_map.54), channel_id=1, source_target_pairs={{0,128},{1,129},{2,130},{3,131},{4,132},{5,133},{6,134},{7,135},{8... | collective-permute-start | bytes 393224 | tf_op jit(solution)/shard_map/ppermute | solution.py:626
  159.4 1.9 %collective-permute-done.8.inflow_ref = f32[256,128]{1,0:T(8,128)S(1)} collective-permute-done((f32[256,128]{1,0:T(8,128)S(1)}, f32[256,128]{1,0:T(8,128)S(1)}, u32[]{:S(2)}, u32[]{:S(2)}) %collective-permute-start.8) | collective-permute-done | bytes 131104 | tf_op jit(solution)/shard_map/ppermute | solution.py:626
  161.3 13.5 %shard_map.55 = f32[3,8,64,256]{3,2,1,0:T(8,128)} custom-call(s32[1]{0:T(128)} %bitcast.wake_ref, f32[3,8,64,256]{3,2,1,0:T(8,128)S(1)} %copy-done.1, f32[3,8,8,256]{3,2,1,0:T(8,128)S(1)} %get-tuple-element.39.tail_ref, f32[3,3,72,256]{3,2,1,0:T(8,128)S(1)} %collective-permute-done.6.low_ref, f32[3,3,72,256]{3,2,1,0:T(8,128)} %collective-permute-done.7.high_ref, ...), custom_call_target="tpu_custom_call" | custom-call | tf_op jit(solution)/shard_map/pallas_call | solution.py:505
  (13 shorter events, 0.1 us)
Async XLA Ops:
  4.3 51.1 %all-to-all-start = ((f32[128,24,128]{2,1,0:T(8,128)}), f32[128,24,128]{2,1,0:T(8,128)}, u32[]{:S(2)}, u32[]{:S(2)}) async-start(f32[128,24,128]{2,1,0:T(8,128)} %bitcast.10), calls=%async_computation | async-start | bytes 3145728 | tf_op jit(solution)/shard_map/all_to_all | solution.py:609
  18.6 28.6 %collective-permute-start.1 = (f32[3,8,2,256]{3,2,1,0:T(2,128)S(1)}, f32[3,8,2,256]{3,2,1,0:T(2,128)S(1)}, u32[]{:S(2)}, u32[]{:S(2)}) collective-permute-start(f32[3,8,2,256]{3,2,1,0:T(2,128)S(1)} %get-tuple-element.46), channel_id=1, source_target_pairs={{0,32},{32,64},{64,96},{96,0},{1,33},{33,65},{65,97},{97,1},{2,34}... | collective-permute-start | bytes 147464 | tf_op jit(solution)/shard_map/ppermute | solution.py:576
  20.1 27.1 %collective-permute-start = (f32[3,8,2,256]{3,2,1,0:T(2,128)S(1)}, f32[3,8,2,256]{3,2,1,0:T(2,128)S(1)}, u32[]{:S(2)}, u32[]{:S(2)}) collective-permute-start(f32[3,8,2,256]{3,2,1,0:T(2,128)S(1)} %get-tuple-element.47), channel_id=1, source_target_pairs={{32,0},{64,32},{96,64},{0,96},{33,1},{65,33},{97,65},{1,97},{34,2}... | collective-permute-start | bytes 147464 | tf_op jit(solution)/shard_map/ppermute | solution.py:581
  48.8 33.4 %copy-start.3 = (f32[3,8,72,256]{3,2,1,0:T(8,128)}, f32[3,8,72,256]{3,2,1,0:T(8,128)S(1)}, u32[]{:S(2)}) copy-start(f32[3,8,72,256]{3,2,1,0:T(8,128)S(1)} %fusion) | copy-start | bytes 5308420
  69.5 49.4 %all-to-all-start.1 = ((f32[128,24,128]{2,1,0:T(8,128)}), f32[128,24,128]{2,1,0:T(8,128)}, u32[]{:S(2)}, u32[]{:S(2)}) async-start(f32[128,24,128]{2,1,0:T(8,128)} %shard_map.51), calls=%async_computation.1 | async-start | bytes 3145728 | tf_op jit(solution)/shard_map/all_to_all | solution.py:617
  82.2 15.0 %collective-permute-start.2 = (f32[3,2,72,256]{3,2,1,0:T(8,128)S(1)}, f32[3,2,72,256]{3,2,1,0:T(8,128)S(1)}, u32[]{:S(2)}, u32[]{:S(2)}) collective-permute-start(f32[3,2,72,256]{3,2,1,0:T(8,128)S(1)} %get-tuple-element.44), channel_id=1, source_target_pairs={{0,1},{1,2},{2,3},{3,4},{4,5},{5,6},{6,7},{7,8},{8,9},{9,10},{10,1... | collective-permute-start | bytes 1327112 | tf_op jit(solution)/shard_map/ppermute | solution.py:576
  83.2 35.7 %copy-start.2 = (f32[1,3]{1,0:T(1,128)S(1)}, f32[1,3]{1,0:T(1,128)}, u32[]{:S(2)}) copy-start(f32[1,3]{1,0:T(1,128)} %drift_ref.1) | copy-start | bytes 40
  83.2 17.5 %collective-permute-start.3 = (f32[3,2,72,256]{3,2,1,0:T(8,128)S(1)}, f32[3,2,72,256]{3,2,1,0:T(8,128)S(1)}, u32[]{:S(2)}, u32[]{:S(2)}) collective-permute-start(f32[3,2,72,256]{3,2,1,0:T(8,128)S(1)} %get-tuple-element.45), channel_id=1, source_target_pairs={{1,0},{2,1},{3,2},{4,3},{5,4},{6,5},{7,6},{8,7},{9,8},{10,9},{11,1... | collective-permute-start | bytes 1327112 | tf_op jit(solution)/shard_map/ppermute | solution.py:581
  122.7 3.2 %collective-permute-start.4 = (f32[72,256]{1,0:T(8,128)S(1)}, f32[72,256]{1,0:T(8,128)S(1)}, u32[]{:S(2)}, u32[]{:S(2)}) collective-permute-start(f32[72,256]{1,0:T(8,128)S(1)} %get-tuple-element.37), channel_id=1, source_target_pairs={{32,0},{64,32},{96,64},{0,96},{33,1},{65,33},{97,65},{1,97},{34,2}... | collective-permute-start | bytes 221192 | tf_op jit(solution)/shard_map/ppermute | solution.py:581
  123.3 5.0 %collective-permute-start.5 = (f32[72,256]{1,0:T(8,128)S(1)}, f32[72,256]{1,0:T(8,128)S(1)}, u32[]{:S(2)}, u32[]{:S(2)}) collective-permute-start(f32[72,256]{1,0:T(8,128)S(1)} %get-tuple-element.38), channel_id=1, source_target_pairs={{0,32},{32,64},{64,96},{96,0},{1,33},{33,65},{65,97},{97,1},{2,34}... | collective-permute-start | bytes 221192 | tf_op jit(solution)/shard_map/ppermute | solution.py:576
  129.6 1.1 copy-start
  130.7 14.3 %collective-permute-start.6 = (f32[3,3,72,256]{3,2,1,0:T(8,128)}, f32[3,3,72,256]{3,2,1,0:T(8,128)S(1)}, u32[]{:S(2)}, u32[]{:S(2)}) collective-permute-start(f32[3,3,72,256]{3,2,1,0:T(8,128)} %get-tuple-element.40), channel_id=1, source_target_pairs={{0,1},{1,2},{2,3},{3,4},{4,5},{5,6},{6,7},{7,8},{8,9},{9,10},{10,1... | collective-permute-start | bytes 1990664 | tf_op jit(solution)/shard_map/ppermute | solution.py:576
  137.1 13.7 %collective-permute-start.7 = (f32[3,3,72,256]{3,2,1,0:T(8,128)}, f32[3,3,72,256]{3,2,1,0:T(8,128)}, u32[]{:S(2)}, u32[]{:S(2)}) collective-permute-start(f32[3,3,72,256]{3,2,1,0:T(8,128)} %get-tuple-element.41), channel_id=1, source_target_pairs={{1,0},{2,1},{3,2},{4,3},{5,4},{6,5},{7,6},{8,7},{9,8},{10,9},{11,1... | collective-permute-start | bytes 1990664 | tf_op jit(solution)/shard_map/ppermute | solution.py:581
  150.8 1.4 copy-start.1
  155.0 6.4 %collective-permute-start.8 = (f32[256,128]{1,0:T(8,128)S(1)}, f32[256,128]{1,0:T(8,128)S(1)}, u32[]{:S(2)}, u32[]{:S(2)}) collective-permute-start(f32[256,128]{1,0:T(8,128)S(1)} %shard_map.54), channel_id=1, source_target_pairs={{0,128},{1,129},{2,130},{3,131},{4,132},{5,133},{6,134},{7,135},{8... | collective-permute-start | bytes 393224 | tf_op jit(solution)/shard_map/ppermute | solution.py:626

commit v2 on v1

--- a/solution.py
+++ b/solution.py
@@ -132,7 +132,7 @@
 
 def plane_kernel(
     owner_ref, in_ref, z_any, y_any, back_any, flip_any, out_ref,
-    plain_ref, z_ref, y_ref, back_ref, flip_ref, sems,
+    plain_ref, turned_ref, z_ref, y_ref, back_ref, flip_ref, sems,
 ):
     n = y_ref.shape[1] // 2
     pairs = ((z_any, z_ref), (y_any, y_ref), (back_any, back_ref), (flip_any, flip_ref))
@@ -157,7 +157,6 @@
     delta = 0.5 * (scale - top_scale)
     copies[0].wait()
     copies[1].wait()
-    copies[3].wait()
     for c in range(3):
         blocks = [
             in_ref[32 * g : 32 * g + 32, 8 * c : 8 * c + 8, :].reshape(n, 128) for g in range(4)
@@ -176,11 +175,15 @@
         imag_cos, imag_sin = value[n:, :n], value[n:, n:]
         plain_ref[c, :n, :] = (real_cos + imag_sin) * sigma
         plain_ref[c, n:, :] = (imag_cos - real_sin) * sigma
-
-        @pl.when(is_packed)
-        def _():
-            turned = jnp.concatenate([real_cos - imag_sin, imag_cos + real_sin], 1)
-            high, low = split(turned)
+        turned_ref[c, :, :n] = real_cos - imag_sin
+        turned_ref[c, :, n:] = imag_cos + real_sin
+
+    copies[3].wait()
+
+    @pl.when(is_packed)
+    def _():
+        for c in range(3):
+            high, low = split(turned_ref[c])
             mirror = product(flip_ref[...], high) + product(flip_ref[...], low)
             plain_ref[c, :n, :] += mirror[:, :n] * delta
             plain_ref[c, n:, :] -= mirror[:, n:] * delta
@@ -215,7 +218,7 @@
 ):
     comps, local_z, local_y, count = out_ref.shape
 
-    def component(c, carry):
+    for c in range(comps):
         parts = []
         for part in range(2):
             chunks = [
@@ -226,9 +229,6 @@
         result = right_product(value, table_ref[...]) + drift_ref[0, c]
         out_ref[c] = result.reshape(local_z, local_y, count)
         speed_ref[c] = result.reshape(local_z, local_y, count)
-        return carry
-
-    lax.fori_loop(0, comps, component, 0)
     for c in range(comps):
         for z in range(local_z):
             row = (c * local_z + z) * RIM
@@ -288,8 +288,9 @@
     @pl.when(wake_ref[0] == 0)
     def _():
         line_ref[...] = jnp.zeros(line_ref.shape, F32)
+        columns = jnp.zeros((72, 128), F32)
         for q in range(planes + 2):
-            columns = jnp.zeros((72, 128), F32)
+            base = 24 * (q % 5)
             for c in range(3):
                 if q < RIM:
                     first, last = low_ref[c, q, :, :128], low_ref[c, q, :, 128:]
@@ -303,19 +304,22 @@
                 else:
                     z = q - RIM - local_z
                     first, last = high_ref[c, z, :, :128], high_ref[c, z, :, 128:]
-                at = 4 * c
-                here = (lane >= at) & (lane < at + 3)
-                columns = jnp.where(here, rotated(last, at + 3), columns)
-                columns = jnp.where(lane == at + 3, rotated(first, at + 3), columns)
+                at = base + 4 * c
+                here = (lane >= at) & (lane < at + 4)
+                ends = jnp.where(lane < 64, first, last)
+                columns = jnp.where(here, rotated(ends, at + 3), columns)
                 if 1 <= q <= planes:
-                    at = 12 + 2 * c
+                    at = base + 12 + 2 * c
                     here = (lane >= at) & (lane < at + 2)
                     columns = jnp.where(
                         here, rotated(field_ref[c, q - 1, :, 128:], at + 2), columns
                     )
-            gap = jnp.zeros((40, 128), F32)
-            whole = jnp.concatenate([columns, columns[:8], gap, columns[64:]], 0)
-            line_ref[24 * q : 24 * q + 24, :] = whole.T[:24]
+            if q % 5 == 4 or q == planes + 1:
+                gap = jnp.zeros((40, 128), F32)
+                whole = jnp.concatenate([columns, columns[:8], gap, columns[64:]], 0)
+                row = 120 * (q // 5)
+                line_ref[row : row + 120, :] = whole.T[:120]
+                columns = jnp.zeros((72, 128), F32)
 
         def line(row, plane):
             return line_ref[pl.ds(24 * plane + row, 16, stride=24), :]
@@ -379,8 +383,11 @@
     is_wake = wake_ref[0] != 0
     entering_lane = is_wake & (lane == 0)
     leaving_lane = is_wake & (lane == 127)
+    inflow_lanes = is_wake & (lane < 2)
     crossing = {o: is_wake & (lane >= 128 - o if o > 0 else lane < -o) for o in (-2, -1, 1, 2)}
     most = fill_speed(speed_ref, tail_ref, low_ref, high_ref, all_ref)
+    for i in range(2):
+        column_ref[i] = inflow_ref[128 * i : 128 * i + 128, :].T
     is_small = TIME_STEP * most < 0.999
 
     def turned(pair, o):
@@ -389,9 +396,6 @@
         return jnp.where(swap, second, first), jnp.where(swap, first, second)
 
     def step(p, small):
-        column_ref[...] = jnp.concatenate(
-            [inflow_ref[pl.ds(16 * p, 16), :], jnp.zeros((112, 128), F32)], 0
-        ).T
         for block in range(72 // size):
             here = slice(size * block, size * block + size)
             kept = slice(8 + size * block, 8 + size * block + size)
@@ -401,7 +405,8 @@
                 row = 8 + size * block + steps
                 return all_ref[c, plane, t, row : row + size, :]
 
-            inflow = column_ref[here, :]
+            inflow = column_ref[p // 8, here, :]
+            turn = 128 - 16 * (p % 8)
             along = []
             for t in range(2):
                 along.append(weights(TIME_STEP * velocity(0, p + 1, t), small))
@@ -420,7 +425,8 @@
             for c in range(3):
                 value = [velocity(c, p + 1, t) for t in range(2)]
                 ahead, behind = list(turned(value, -1)), list(turned(value, 1))
-                behind[0] = jnp.where(entering_lane, rotated(inflow, -(4 * c + 2)), behind[0])
+                entering = pltpu.roll(inflow, turn - (4 * c + 2), 1)
+                behind[0] = jnp.where(entering_lane, entering, behind[0])
                 ahead[1] = jnp.where(leaving_lane, value[1], ahead[1])
                 strength = []
                 for t in range(2):
@@ -434,7 +440,8 @@
                         )
                     )
                 total = [strength[t] * along[t][0] for t in range(2)]
-                total[0] = total[0] + jnp.where(lane < 2, rotated(inflow, -4 * c), 0.0)
+                passed_on = pltpu.roll(inflow, turn - 4 * c, 1)
+                total[0] = total[0] + jnp.where(inflow_lanes, passed_on, 0.0)
                 for o in (-2, -1, 1, 2):
                     pair = turned([strength[t] * along[t][o] for t in range(2)], o)
                     total = [total[t] + pair[t] for t in range(2)]
@@ -528,7 +535,7 @@
 def solve_plane(spectrum, owner, tables):
     count = tables[3].shape[1]
     args = (owner.reshape(1), spectrum, *tables)
-    scratch = [pltpu.VMEM((3, 2 * count, count), F32)]
+    scratch = [pltpu.VMEM((3, 2 * count, count), F32), pltpu.VMEM((3, count, 2 * count), F32)]
     scratch += [pltpu.VMEM(t.shape, t.dtype) for t in tables]
     scratch += [pltpu.SemaphoreType.DMA((len(tables),))]
     far = (2, 3, 4, 5)
@@ -561,7 +568,7 @@
     lanes, planes = count // 128, local_z + 4
     scratch = [
         pltpu.VMEM((comps, planes + 2, lanes, local_y + 24, 128), F32),
-        pltpu.VMEM((128, 128), F32),
+        pltpu.VMEM((2, 128, 128), F32),
         pltpu.VMEM((comps, lanes, local_y + 16, 128), F32),
         pltpu.VMEM((5, lanes, local_y + 16, 128), F32),
         pltpu.VMEM((comps, planes, lanes, local_y, 128), F32),
@@ -604,7 +611,7 @@
     axes = ("gy", "gz")
     spectrum = forward_lines(field)
     start = lax.axis_index("grp") * 0
-    spectrum, start, halo_field = lax.optimization_barrier((spectrum, start, field))
+    spectrum, start, halo_field, wake = lax.optimization_barrier((spectrum, start, field, wake))
     spectrum = spectrum.reshape(groups, 24, 128)
     spectrum = lax.all_to_all(spectrum, axes, split_axis=0, concat_axis=0, tiled=True)
     wide = wider_rows(halo_field)
@@ -623,7 +630,7 @@
     tail, up, down = with_edges(speed, above, below)
     low, high = from_before(up, "gz"), from_after(down, "gz")
     inflow = inflow_columns(wake, speed, tail, low, high, wide)
-    inflow = lax.ppermute(inflow, "grp", [(0, 1)])
+    inflow = lax.ppermute(inflow, "grp", [(0, 1), (1, 0)])
     result = wake_step(wake, speed, tail, low, high, wide, inflow)
     return (result[None], velocity[None])
 

time: 175 us -> 169 us (0.966)
  Pallas kernels: 39 us -> 32.9 us
  waiting for transfers between devices: 66.4 us -> 70 us
  local copies, waits for them, and re-layouts: 3.68 us -> 1.13 us
    pallas_call x6, Pallas kernels: 39 us -> 32.9 us  [call(): pl.pallas_call(kernel, out_shape=outs, in_specs=specs, out_specs=[pl.Bloc...]
    ppermute x1, waiting for transfers between devices: 1.92 us -> 5.85 us  [body(): inflow = lax.ppermute(inflow, 'grp', [(0, 1), (1, 0)])]
    unnamed x8 -> x4, local copies, waits for them, and re-layouts: 2.56 us -> 0.01 us
  transfers between devices with their start and end apart: 11 -> 11, of which waited for: 10 -> 10; matrix products, arithmetic and copies ran while one was open for 13% -> 14% of each run, Pallas kernels for 0% -> 0%
where the time goes in v2:
time: 169 us; the launch traced here: 168 us
  waiting for transfers between devices  70 us (41%)
  starting transfers between devices  41.7 us (25%)
  Pallas kernels  32.9 us (19%)
  other arithmetic  21.8 us (13%)
    pallas_call x6, Pallas kernels, call(): pl.pallas_call(kernel, out_shape=outs, in_specs=specs, out_specs=[pl.Bloc...  32.9 us
    ppermute x4, waiting for transfers between devices, from_before(): lax.ppermute(value, axis, [(i, (i + 1) % count) for i in range(count)])  30.2 us
    all_to_all x2, starting transfers between devices, body(): lax.all_to_all(spectrum, axes, split_axis=0, concat_axis=0, tiled=True)  25.5 us
    all_to_all x2, waiting for transfers between devices, body(): lax.all_to_all(spectrum, axes, split_axis=0, concat_axis=0, tiled=True)  23.1 us
    convert_element_type x3, other arithmetic, tripled(): high = high.astype(BF16)  14 us
    ppermute x4, waiting for transfers between devices, from_after(): lax.ppermute(value, axis, [((i + 1) % count, i) for i in range(count)])  11 us
    ppermute x4, starting transfers between devices, from_before(): lax.ppermute(value, axis, [(i, (i + 1) % count) for i in range(count)])  9.71 us
    ppermute x1, waiting for transfers between devices, body(): inflow = lax.ppermute(inflow, 'grp', [(0, 1), (1, 0)])  5.85 us
  transfers between devices with their start and end apart: 11, of which 10 were waited for; matrix products, arithmetic and copies ran while one was open for 14% of the time, Pallas kernels for 0%

profile of v2, /device:TPU:31, one launch (start us, length us, event | category | flops | bytes accessed | tf_op | source)
XLA Modules:
  0.0 168.4 jit_solution(15533483735758271491)
XLA Ops:
  0.6 3.6 %shard_map.50 = f32[3072,128]{1,0:T(8,128)} custom-call(f32[3,8,64,256]{3,2,1,0:T(8,128)} %bitcast.7, bf16[2,256,256]{2,1,0:T(8,128)(2,1)} %constant.213.clone.table_any), custom_call_target="tpu_custom_call" | custom-call | tf_op jit(solution)/shard_map/pallas_call | solution.py:512
  4.3 13.3 %all-to-all-start = ((f32[128,24,128]{2,1,0:T(8,128)}), f32[128,24,128]{2,1,0:T(8,128)}, u32[]{:S(2)}, u32[]{:S(2)}) async-start(f32[128,24,128]{2,1,0:T(8,128)} %bitcast.10), calls=%async_computation | async-start | bytes 3145728 | tf_op jit(solution)/shard_map/all_to_all | solution.py:616
  17.5 1.1 fusion.49
  18.6 1.5 collective-permute-start.1
  20.1 2.5 %collective-permute-start = (f32[3,8,2,256]{3,2,1,0:T(2,128)S(1)}, f32[3,8,2,256]{3,2,1,0:T(2,128)S(1)}, u32[]{:S(2)}, u32[]{:S(2)}) collective-permute-start(f32[3,8,2,256]{3,2,1,0:T(2,128)S(1)} %get-tuple-element.49), channel_id=1, source_target_pairs={{32,0},{64,32},{96,64},{0,96},{33,1},{65,33},{97,65},{1,97},{34,2}... | collective-permute-start | bytes 147464 | tf_op jit(solution)/shard_map/ppermute | solution.py:588
  22.7 2.5 %reduce-precision_convert_fusion.2 = (bf16[256,512]{1,0:T(8,128)(2,1)S(1)}, bf16[256,512]{1,0:T(8,128)(2,1)S(1)}) fusion(s32[512]{0:T(512)S(1)} %get-tuple-element.61, s32[512]{0:T(512)S(1)} %get-tuple-element.75, pred[512]{0:T(512)(128)(4,1)S(1)} %get-tuple-element.66, s32[256]{0:T(256)S(1)} %get-tuple-element.70, pred[512]{0:T(512)(128)(4,1)S(1)} %get-tuple-element.62), kind=kLoop, calls=%fused_computation.82 | loop fusion | flops 2621440 | bytes 530432 | tf_op jit(solution)/shard_map/convert_element_type | solution.py:77
  25.3 1.0 pad_maximum_fusion.3.y_any
  26.2 0.8 fusion.40.flip_any
  27.1 1.5 reduce-precision_convert_fusion.3
  28.6 10.0 %reduce-precision_convert_fusion = (bf16[512,512]{1,0:T(8,128)(2,1)S(1)}, bf16[512,512]{1,0:T(8,128)(2,1)S(1)}, bf16[512,512]{1,0:T(8,128)(2,1)S(1)}, bf16[512,512]{1,0:T(8,128)(2,1)S(1)}) fusion(pred[512]{0:T(512)(128)(4,1)S(1)} %get-tuple-element.62, s32[512]{0:T(512)S(1)} %get-tuple-element.60, s32[512]{0:T(512)S(1)} %get-tuple-element.77, ...), kind=kLoop, calls=%fused_computation.43 | loop fusion | flops 29622272 | bytes 2116096 | tf_op jit(solution)/shard_map/convert_element_type | solution.py:77
  38.6 1.2 pad_maximum_fusion.2.back_any
  39.9 1.2 pad_maximum_fusion.1.z_any
  41.1 6.1 %collective-permute-done.1 = f32[3,8,2,256]{3,2,1,0:T(2,128)S(1)} collective-permute-done((f32[3,8,2,256]{3,2,1,0:T(2,128)S(1)}, f32[3,8,2,256]{3,2,1,0:T(2,128)S(1)}, u32[]{:S(2)}, u32[]{:S(2)}) %collective-permute-start.1) | collective-permute-done | bytes 49184 | tf_op jit(solution)/shard_map/ppermute | solution.py:583
  47.2 0.0 collective-permute-done
  47.2 1.6 fusion
  48.8 0.0 copy-start.1
  48.8 6.6 %all-to-all-done.in_ref = f32[128,24,128]{2,1,0:T(8,128)} async-done(((f32[128,24,128]{2,1,0:T(8,128)}), f32[128,24,128]{2,1,0:T(8,128)}, u32[]{:S(2)}, u32[]{:S(2)}) %all-to-all-start) | async-done | bytes 1572896 | tf_op jit(solution)/shard_map/all_to_all | solution.py:616
  55.4 11.5 %shard_map.51 = f32[128,24,128]{2,1,0:T(8,128)} custom-call(s32[1]{0:T(128)} %bitcast.2.owner_ref, f32[128,24,128]{2,1,0:T(8,128)} %all-to-all-done.in_ref, bf16[512,1536]{1,0:T(8,128)(2,1)} %pad_maximum_fusion.1.z_any, bf16[768,512]{1,0:T(8,128)(2,1)} %pad_maximum_fusion.3.y_any, bf16[512,1536]{1,0:T(8,128)(2,1)} %pad_maximum_fusion.2.back_any, ...), custom_call_target="tpu_custom_call" | custom-call | tf_op jit(solution)/shard_map/pallas_call | solution.py:512
  66.9 12.3 %all-to-all-start.1 = ((f32[128,24,128]{2,1,0:T(8,128)}), f32[128,24,128]{2,1,0:T(8,128)}, u32[]{:S(2)}, u32[]{:S(2)}) async-start(f32[128,24,128]{2,1,0:T(8,128)} %shard_map.51), calls=%async_computation.1 | async-start | bytes 3145728 | tf_op jit(solution)/shard_map/all_to_all | solution.py:624
  79.2 0.0 copy-done.1
  79.2 0.1 fusion.48
  79.3 0.9 collective-permute-start.2
  80.2 0.0 copy-start
  80.2 0.0 collective-permute-start.3
  80.2 14.0 %collective-permute-done.2 = f32[3,2,72,256]{3,2,1,0:T(8,128)S(1)} collective-permute-done((f32[3,2,72,256]{3,2,1,0:T(8,128)S(1)}, f32[3,2,72,256]{3,2,1,0:T(8,128)S(1)}, u32[]{:S(2)}, u32[]{:S(2)}) %collective-permute-start.2) | collective-permute-done | bytes 442400 | tf_op jit(solution)/shard_map/ppermute | solution.py:583
  94.3 3.4 %collective-permute-done.3 = f32[3,2,72,256]{3,2,1,0:T(8,128)S(1)} collective-permute-done((f32[3,2,72,256]{3,2,1,0:T(8,128)S(1)}, f32[3,2,72,256]{3,2,1,0:T(8,128)S(1)}, u32[]{:S(2)}, u32[]{:S(2)}) %collective-permute-start.3) | collective-permute-done | bytes 442400 | tf_op jit(solution)/shard_map/ppermute | solution.py:588
  97.7 1.7 %pad_maximum_fusion.field_ref = f32[3,12,72,256]{3,2,1,0:T(8,128)S(1)} fusion(f32[3,2,72,256]{3,2,1,0:T(8,128)S(1)} %collective-permute-done.3, f32[3,8,72,256]{3,2,1,0:T(8,128)} %copy-done.1, f32[3,2,72,256]{3,2,1,0:T(8,128)S(1)} %collective-permute-done.2), kind=kLoop, calls=%fused_computation.12 | loop fusion | flops 1327104 | bytes 5308416 | tf_op jit(solution)/shard_map/concatenate | solution.py:601
  99.4 16.5 %all-to-all-done.1 = f32[128,24,128]{2,1,0:T(8,128)} async-done(((f32[128,24,128]{2,1,0:T(8,128)}), f32[128,24,128]{2,1,0:T(8,128)}, u32[]{:S(2)}, u32[]{:S(2)}) %all-to-all-start.1) | async-done | bytes 1572896 | tf_op jit(solution)/shard_map/all_to_all | solution.py:624
  115.9 0.0 copy-done
  115.9 3.6 %shard_map.52 = (f32[3,8,64,256]{3,2,1,0:T(8,128)}, f32[3,8,64,256]{3,2,1,0:T(8,128)S(1)}, f32[72,256]{1,0:T(8,128)S(1)}, f32[72,256]{1,0:T(8,128)S(1)}) custom-call(f32[3072,128]{1,0:T(8,128)} %bitcast.4.in_ref, bf16[768,256]{1,0:T(8,128)(2,1)S(1)} %pad_maximum_fusion.4.table_ref, f32[1,3]{1,0:T(1,128)S(1)} %copy-done), custom_call_target="tpu_custom_call" | custom-call | tf_op jit(solution)/shard_map/pallas_call | solution.py:512
  119.5 0.6 collective-permute-start.4
  120.1 0.8 collective-permute-start.5
  120.9 1.7 %collective-permute-done.4.above_ref = f32[72,256]{1,0:T(8,128)S(1)} collective-permute-done((f32[72,256]{1,0:T(8,128)S(1)}, f32[72,256]{1,0:T(8,128)S(1)}, u32[]{:S(2)}, u32[]{:S(2)}) %collective-permute-start.4) | collective-permute-done | bytes 73760 | tf_op jit(solution)/shard_map/ppermute | solution.py:588
  122.7 2.4 %collective-permute-done.5.below_ref = f32[72,256]{1,0:T(8,128)S(1)} collective-permute-done((f32[72,256]{1,0:T(8,128)S(1)}, f32[72,256]{1,0:T(8,128)S(1)}, u32[]{:S(2)}, u32[]{:S(2)}) %collective-permute-start.5) | collective-permute-done | bytes 73760 | tf_op jit(solution)/shard_map/ppermute | solution.py:583
  125.1 0.1 shard_map.53
  125.3 6.5 %collective-permute-start.6 = (f32[3,3,72,256]{3,2,1,0:T(8,128)S(1)}, f32[3,3,72,256]{3,2,1,0:T(8,128)S(1)}, u32[]{:S(2)}, u32[]{:S(2)}) collective-permute-start(f32[3,3,72,256]{3,2,1,0:T(8,128)S(1)} %get-tuple-element.42), channel_id=1, source_target_pairs={{0,1},{1,2},{2,3},{3,4},{4,5},{5,6},{6,7},{7,8},{8,9},{9,10},{10,1... | collective-permute-start | bytes 1990664 | tf_op jit(solution)/shard_map/ppermute | solution.py:583
  131.7 0.0 collective-permute-start.7
  131.7 7.6 %collective-permute-done.6.low_ref = f32[3,3,72,256]{3,2,1,0:T(8,128)S(1)} collective-permute-done((f32[3,3,72,256]{3,2,1,0:T(8,128)S(1)}, f32[3,3,72,256]{3,2,1,0:T(8,128)S(1)}, u32[]{:S(2)}, u32[]{:S(2)}) %collective-permute-start.6) | collective-permute-done | bytes 663584 | tf_op jit(solution)/shard_map/ppermute | solution.py:583
  139.3 5.8 %collective-permute-done.7.high_ref = f32[3,3,72,256]{3,2,1,0:T(8,128)S(1)} collective-permute-done((f32[3,3,72,256]{3,2,1,0:T(8,128)S(1)}, f32[3,3,72,256]{3,2,1,0:T(8,128)S(1)}, u32[]{:S(2)}, u32[]{:S(2)}) %collective-permute-start.7) | collective-permute-done | bytes 663584 | tf_op jit(solution)/shard_map/ppermute | solution.py:588
  145.1 1.1 shard_map.54
  146.3 3.4 %collective-permute-start.8 = (f32[256,128]{1,0:T(8,128)S(1)}, f32[256,128]{1,0:T(8,128)S(1)}, u32[]{:S(2)}, u32[]{:S(2)}) collective-permute-start(f32[256,128]{1,0:T(8,128)S(1)} %shard_map.54), channel_id=1, source_target_pairs={{0,128},{128,0},{1,129},{129,1},{2,130},{130,2},{3,131},{131,3},{4... | collective-permute-start | bytes 393224 | tf_op jit(solution)/shard_map/ppermute | solution.py:633
  149.6 5.8 %collective-permute-done.8.inflow_ref = f32[256,128]{1,0:T(8,128)S(1)} collective-permute-done((f32[256,128]{1,0:T(8,128)S(1)}, f32[256,128]{1,0:T(8,128)S(1)}, u32[]{:S(2)}, u32[]{:S(2)}) %collective-permute-start.8) | collective-permute-done | bytes 131104 | tf_op jit(solution)/shard_map/ppermute | solution.py:633
  155.5 12.9 %shard_map.55 = f32[3,8,64,256]{3,2,1,0:T(8,128)} custom-call(s32[1]{0:T(128)} %bitcast.1.wake_ref, f32[3,8,64,256]{3,2,1,0:T(8,128)S(1)} %get-tuple-element.38.speed_ref, f32[3,8,8,256]{3,2,1,0:T(8,128)S(1)} %get-tuple-element.41.tail_ref, f32[3,3,72,256]{3,2,1,0:T(8,128)S(1)} %collective-permute-done.6.low_ref, ...), custom_call_target="tpu_custom_call" | custom-call | tf_op jit(solution)/shard_map/pallas_call | solution.py:512
  (13 shorter events, 0.1 us)
Async XLA Ops:
  4.3 51.1 %all-to-all-start = ((f32[128,24,128]{2,1,0:T(8,128)}), f32[128,24,128]{2,1,0:T(8,128)}, u32[]{:S(2)}, u32[]{:S(2)}) async-start(f32[128,24,128]{2,1,0:T(8,128)} %bitcast.10), calls=%async_computation | async-start | bytes 3145728 | tf_op jit(solution)/shard_map/all_to_all | solution.py:616
  18.6 28.6 %collective-permute-start.1 = (f32[3,8,2,256]{3,2,1,0:T(2,128)S(1)}, f32[3,8,2,256]{3,2,1,0:T(2,128)S(1)}, u32[]{:S(2)}, u32[]{:S(2)}) collective-permute-start(f32[3,8,2,256]{3,2,1,0:T(2,128)S(1)} %get-tuple-element.48), channel_id=1, source_target_pairs={{0,32},{32,64},{64,96},{96,0},{1,33},{33,65},{65,97},{97,1},{2,34}... | collective-permute-start | bytes 147464 | tf_op jit(solution)/shard_map/ppermute | solution.py:583
  20.1 27.1 %collective-permute-start = (f32[3,8,2,256]{3,2,1,0:T(2,128)S(1)}, f32[3,8,2,256]{3,2,1,0:T(2,128)S(1)}, u32[]{:S(2)}, u32[]{:S(2)}) collective-permute-start(f32[3,8,2,256]{3,2,1,0:T(2,128)S(1)} %get-tuple-element.49), channel_id=1, source_target_pairs={{32,0},{64,32},{96,64},{0,96},{33,1},{65,33},{97,65},{1,97},{34,2}... | collective-permute-start | bytes 147464 | tf_op jit(solution)/shard_map/ppermute | solution.py:588
  48.8 30.4 %copy-start.1 = (f32[3,8,72,256]{3,2,1,0:T(8,128)}, f32[3,8,72,256]{3,2,1,0:T(8,128)S(1)}, u32[]{:S(2)}) copy-start(f32[3,8,72,256]{3,2,1,0:T(8,128)S(1)} %fusion) | copy-start | bytes 5308420
  66.9 49.0 %all-to-all-start.1 = ((f32[128,24,128]{2,1,0:T(8,128)}), f32[128,24,128]{2,1,0:T(8,128)}, u32[]{:S(2)}, u32[]{:S(2)}) async-start(f32[128,24,128]{2,1,0:T(8,128)} %shard_map.51), calls=%async_computation.1 | async-start | bytes 3145728 | tf_op jit(solution)/shard_map/all_to_all | solution.py:624
  79.3 15.0 %collective-permute-start.2 = (f32[3,2,72,256]{3,2,1,0:T(8,128)S(1)}, f32[3,2,72,256]{3,2,1,0:T(8,128)S(1)}, u32[]{:S(2)}, u32[]{:S(2)}) collective-permute-start(f32[3,2,72,256]{3,2,1,0:T(8,128)S(1)} %get-tuple-element.46), channel_id=1, source_target_pairs={{0,1},{1,2},{2,3},{3,4},{4,5},{5,6},{6,7},{7,8},{8,9},{9,10},{10,1... | collective-permute-start | bytes 1327112 | tf_op jit(solution)/shard_map/ppermute | solution.py:583
  80.2 35.7 %copy-start = (f32[1,3]{1,0:T(1,128)S(1)}, f32[1,3]{1,0:T(1,128)}, u32[]{:S(2)}) copy-start(f32[1,3]{1,0:T(1,128)} %drift_ref.1) | copy-start | bytes 40
  80.2 17.5 %collective-permute-start.3 = (f32[3,2,72,256]{3,2,1,0:T(8,128)S(1)}, f32[3,2,72,256]{3,2,1,0:T(8,128)S(1)}, u32[]{:S(2)}, u32[]{:S(2)}) collective-permute-start(f32[3,2,72,256]{3,2,1,0:T(8,128)S(1)} %get-tuple-element.47), channel_id=1, source_target_pairs={{1,0},{2,1},{3,2},{4,3},{5,4},{6,5},{7,6},{8,7},{9,8},{10,9},{11,1... | collective-permute-start | bytes 1327112 | tf_op jit(solution)/shard_map/ppermute | solution.py:588
  119.5 3.2 %collective-permute-start.4 = (f32[72,256]{1,0:T(8,128)S(1)}, f32[72,256]{1,0:T(8,128)S(1)}, u32[]{:S(2)}, u32[]{:S(2)}) collective-permute-start(f32[72,256]{1,0:T(8,128)S(1)} %get-tuple-element.39), channel_id=1, source_target_pairs={{32,0},{64,32},{96,64},{0,96},{33,1},{65,33},{97,65},{1,97},{34,2}... | collective-permute-start | bytes 221192 | tf_op jit(solution)/shard_map/ppermute | solution.py:588
  120.1 5.0 %collective-permute-start.5 = (f32[72,256]{1,0:T(8,128)S(1)}, f32[72,256]{1,0:T(8,128)S(1)}, u32[]{:S(2)}, u32[]{:S(2)}) collective-permute-start(f32[72,256]{1,0:T(8,128)S(1)} %get-tuple-element.40), channel_id=1, source_target_pairs={{0,32},{32,64},{64,96},{96,0},{1,33},{33,65},{65,97},{97,1},{2,34}... | collective-permute-start | bytes 221192 | tf_op jit(solution)/shard_map/ppermute | solution.py:583
  125.3 14.1 %collective-permute-start.6 = (f32[3,3,72,256]{3,2,1,0:T(8,128)S(1)}, f32[3,3,72,256]{3,2,1,0:T(8,128)S(1)}, u32[]{:S(2)}, u32[]{:S(2)}) collective-permute-start(f32[3,3,72,256]{3,2,1,0:T(8,128)S(1)} %get-tuple-element.42), channel_id=1, source_target_pairs={{0,1},{1,2},{2,3},{3,4},{4,5},{5,6},{6,7},{7,8},{8,9},{9,10},{10,1... | collective-permute-start | bytes 1990664 | tf_op jit(solution)/shard_map/ppermute | solution.py:583
  131.7 13.4 %collective-permute-start.7 = (f32[3,3,72,256]{3,2,1,0:T(8,128)S(1)}, f32[3,3,72,256]{3,2,1,0:T(8,128)S(1)}, u32[]{:S(2)}, u32[]{:S(2)}) collective-permute-start(f32[3,3,72,256]{3,2,1,0:T(8,128)S(1)} %get-tuple-element.43), channel_id=1, source_target_pairs={{1,0},{2,1},{3,2},{4,3},{5,4},{6,5},{7,6},{8,7},{9,8},{10,9},{11,1... | collective-permute-start | bytes 1990664 | tf_op jit(solution)/shard_map/ppermute | solution.py:588
  146.3 9.2 %collective-permute-start.8 = (f32[256,128]{1,0:T(8,128)S(1)}, f32[256,128]{1,0:T(8,128)S(1)}, u32[]{:S(2)}, u32[]{:S(2)}) collective-permute-start(f32[256,128]{1,0:T(8,128)S(1)} %shard_map.54), channel_id=1, source_target_pairs={{0,128},{128,0},{1,129},{129,1},{2,130},{130,2},{3,131},{131,3},{4... | collective-permute-start | bytes 393224 | tf_op jit(solution)/shard_map/ppermute | solution.py:633

commit v3 on v2

--- a/solution.py
+++ b/solution.py
@@ -131,14 +131,16 @@
 
 
 def plane_kernel(
-    owner_ref, in_ref, z_any, y_any, back_any, flip_any, out_ref,
-    plain_ref, turned_ref, z_ref, y_ref, back_ref, flip_ref, sems,
+    owner_ref, in_any, z_any, y_any, back_any, flip_any, out_ref,
+    in_ref, plain_ref, turned_ref, z_ref, y_ref, back_ref, flip_ref, sems,
 ):
     n = y_ref.shape[1] // 2
-    pairs = ((z_any, z_ref), (y_any, y_ref), (back_any, back_ref), (flip_any, flip_ref))
+    pairs = (
+        (z_any, z_ref), (y_any, y_ref), (back_any, back_ref), (flip_any, flip_ref), (in_any, in_ref)
+    )
     copies = [pltpu.make_async_copy(s, d, sems.at[i]) for i, (s, d) in enumerate(pairs)]
-    for copy in copies:
-        copy.start()
+    for i in (0, 4, 1, 2, 3):
+        copies[i].start()
     owner = owner_ref[0]
     is_packed = owner == 0
     low_lanes = lax.broadcasted_iota(jnp.int32, (n, 128), 1) < 64
@@ -156,6 +158,7 @@
     sigma = jnp.where(is_packed, 0.5 * (scale + top_scale), scale)
     delta = 0.5 * (scale - top_scale)
     copies[0].wait()
+    copies[4].wait()
     copies[1].wait()
     for c in range(3):
         blocks = [
@@ -214,7 +217,7 @@
 
 
 def streamwise_backward(
-    in_ref, table_ref, drift_ref, out_ref, speed_ref, low_ref, high_ref
+    in_ref, table_ref, drift_ref, out_ref, low_ref, high_ref
 ):
     comps, local_z, local_y, count = out_ref.shape
 
@@ -228,7 +231,6 @@
         value = jnp.concatenate(parts, 0).T
         result = right_product(value, table_ref[...]) + drift_ref[0, c]
         out_ref[c] = result.reshape(local_z, local_y, count)
-        speed_ref[c] = result.reshape(local_z, local_y, count)
     for c in range(comps):
         for z in range(local_z):
             row = (c * local_z + z) * RIM
@@ -345,8 +347,10 @@
                 strength[1] * shift[1][2],
                 line(4 * c + 2, 1),
             )
-            for i, row in enumerate(rows):
-                out_ref[pl.ds(4 * c + i, 16, stride=16), :] = row
+            for i in range(2):
+                out_ref[pl.ds(2 * planes * c + i, planes, stride=2), :] = rows[i][:planes]
+            first = 6 * planes + planes * c
+            out_ref[first : first + planes, :] = rows[2][:planes]
 
 
 def fill_speed(speed_ref, tail_ref, low_ref, high_ref, all_ref):
@@ -373,9 +377,11 @@
 
 
 def wake_kernel(
-    wake_ref, speed_ref, tail_ref, low_ref, high_ref, field_ref, inflow_ref, out_ref,
-    all_ref, column_ref, moved_ref, across_ref, lateral_ref, upward_ref,
+    wake_ref, speed_ref, tail_ref, low_ref, high_ref, field_ref, inflow_ref, out_ref, speed_any,
+    all_ref, column_ref, moved_ref, across_ref, lateral_ref, upward_ref, sem,
 ):
+    copy = pltpu.make_async_copy(speed_ref, speed_any, sem)
+    copy.start()
     planes = field_ref.shape[1]
     local_z, local_y = out_ref.shape[1], out_ref.shape[2]
     size = 72
@@ -386,8 +392,8 @@
     inflow_lanes = is_wake & (lane < 2)
     crossing = {o: is_wake & (lane >= 128 - o if o > 0 else lane < -o) for o in (-2, -1, 1, 2)}
     most = fill_speed(speed_ref, tail_ref, low_ref, high_ref, all_ref)
-    for i in range(2):
-        column_ref[i] = inflow_ref[128 * i : 128 * i + 128, :].T
+    missing = 128 - inflow_ref.shape[0]
+    column_ref[...] = jnp.concatenate([inflow_ref[...], jnp.zeros((missing, 128), F32)], 0).T
     is_small = TIME_STEP * most < 0.999
 
     def turned(pair, o):
@@ -405,8 +411,7 @@
                 row = 8 + size * block + steps
                 return all_ref[c, plane, t, row : row + size, :]
 
-            inflow = column_ref[p // 8, here, :]
-            turn = 128 - 16 * (p % 8)
+            inflow = column_ref[here, :]
             along = []
             for t in range(2):
                 along.append(weights(TIME_STEP * velocity(0, p + 1, t), small))
@@ -425,7 +430,7 @@
             for c in range(3):
                 value = [velocity(c, p + 1, t) for t in range(2)]
                 ahead, behind = list(turned(value, -1)), list(turned(value, 1))
-                entering = pltpu.roll(inflow, turn - (4 * c + 2), 1)
+                entering = pltpu.roll(inflow, 128 - (6 + c) * planes - p, 1)
                 behind[0] = jnp.where(entering_lane, entering, behind[0])
                 ahead[1] = jnp.where(leaving_lane, value[1], ahead[1])
                 strength = []
@@ -440,7 +445,7 @@
                         )
                     )
                 total = [strength[t] * along[t][0] for t in range(2)]
-                passed_on = pltpu.roll(inflow, turn - 4 * c, 1)
+                passed_on = pltpu.roll(inflow, 128 - 2 * planes * c - 2 * p, 1)
                 total[0] = total[0] + jnp.where(inflow_lanes, passed_on, 0.0)
                 for o in (-2, -1, 1, 2):
                     pair = turned([strength[t] * along[t][o] for t in range(2)], o)
@@ -500,9 +505,10 @@
         return carry
 
     lax.fori_loop(0, local_z, gather, 0)
-
-
-def call(kernel, shapes, args, smem=(), far=(), scratch=(), limit=24):
+    copy.wait()
+
+
+def call(kernel, shapes, args, smem=(), far=(), far_out=(), scratch=(), limit=24):
     single = not isinstance(shapes, list)
     outs = [jax.ShapeDtypeStruct(s, F32) for s in ([shapes] if single else shapes)]
     def space(i):
@@ -513,7 +519,10 @@
         kernel,
         out_shape=outs,
         in_specs=specs,
-        out_specs=[pl.BlockSpec(memory_space=pltpu.VMEM) for _ in outs],
+        out_specs=[
+            pl.BlockSpec(memory_space=pltpu.HBM if i in far_out else pltpu.VMEM)
+            for i in range(len(outs))
+        ],
         scratch_shapes=list(scratch),
         compiler_params=pltpu.CompilerParams(vmem_limit_bytes=limit * 1024 * 1024),
     )(*args)
@@ -535,10 +544,11 @@
 def solve_plane(spectrum, owner, tables):
     count = tables[3].shape[1]
     args = (owner.reshape(1), spectrum, *tables)
-    scratch = [pltpu.VMEM((3, 2 * count, count), F32), pltpu.VMEM((3, count, 2 * count), F32)]
+    scratch = [pltpu.VMEM(spectrum.shape, F32)]
+    scratch += [pltpu.VMEM((3, 2 * count, count), F32), pltpu.VMEM((3, count, 2 * count), F32)]
     scratch += [pltpu.VMEM(t.shape, t.dtype) for t in tables]
-    scratch += [pltpu.SemaphoreType.DMA((len(tables),))]
-    far = (2, 3, 4, 5)
+    scratch += [pltpu.SemaphoreType.DMA((len(tables) + 1,))]
+    far = (1, 2, 3, 4, 5)
     return call(
         plane_kernel, spectrum.shape, args, smem=(0,), far=far, scratch=scratch, limit=54
     )
@@ -546,7 +556,7 @@
 
 def backward_lines(spectrum, drift, table, shape):
     edge = (shape[0] * shape[1] * RIM, shape[3])
-    shapes = [shape, shape, edge, edge]
+    shapes = [shape, edge, edge]
     return call(streamwise_backward, shapes, (spectrum, table, drift), smem=(2,))
 
 
@@ -560,7 +570,8 @@
 def inflow_columns(wake, speed, tail, low, high, field):
     args = (wake, speed, tail, low, high, field)
     scratch = [pltpu.VMEM((24 * (field.shape[1] + 6), 128), F32)]
-    return call(inflow_kernel, (256, 128), args, smem=(0,), scratch=scratch)
+    shape = (9 * field.shape[1] + 4, 128)
+    return call(inflow_kernel, shape, args, smem=(0,), scratch=scratch)
 
 
 def wake_step(wake, speed, tail, low, high, field, inflow):
@@ -568,14 +579,16 @@
     lanes, planes = count // 128, local_z + 4
     scratch = [
         pltpu.VMEM((comps, planes + 2, lanes, local_y + 24, 128), F32),
-        pltpu.VMEM((2, 128, 128), F32),
+        pltpu.VMEM((128, 128), F32),
         pltpu.VMEM((comps, lanes, local_y + 16, 128), F32),
         pltpu.VMEM((5, lanes, local_y + 16, 128), F32),
         pltpu.VMEM((comps, planes, lanes, local_y, 128), F32),
         pltpu.VMEM((5, planes, lanes, local_y, 128), F32),
+        pltpu.SemaphoreType.DMA,
     ]
     args = (wake, speed, tail, low, high, field, inflow)
-    return call(wake_kernel, speed.shape, args, smem=(0,), scratch=scratch)
+    shapes = [speed.shape, speed.shape]
+    return call(wake_kernel, shapes, args, smem=(0,), far_out=(1,), scratch=scratch)
 
 
 def from_before(value, axis):
@@ -625,13 +638,13 @@
     wide = wider_planes(wide)
     spectrum, wide = lax.optimization_barrier((spectrum, wide))
     spectrum = spectrum.reshape(groups * 24, 128)
-    velocity, speed, first, last = backward_lines(spectrum, wind, streamwise, field.shape)
+    speed, first, last = backward_lines(spectrum, wind, streamwise, field.shape)
     above, below = from_after(first, "gy"), from_before(last, "gy")
     tail, up, down = with_edges(speed, above, below)
     low, high = from_before(up, "gz"), from_after(down, "gz")
     inflow = inflow_columns(wake, speed, tail, low, high, wide)
-    inflow = lax.ppermute(inflow, "grp", [(0, 1), (1, 0)])
-    result = wake_step(wake, speed, tail, low, high, wide, inflow)
+    inflow = lax.ppermute(inflow, "grp", [(0, 1)])
+    result, velocity = wake_step(wake, speed, tail, low, high, wide, inflow)
     return (result[None], velocity[None])
 
 

time: 169 us -> 164 us (0.970)
  waiting for transfers between devices: 70 us -> 65.4 us
  Pallas kernels: 32.9 us -> 31.1 us
  starting transfers between devices: 41.7 us -> 43.4 us
    ppermute x1, waiting for transfers between devices: 5.85 us -> 1.23 us  [body(): inflow = lax.ppermute(inflow, 'grp', [(0, 1)])]
    pallas_call x6, Pallas kernels: 32.9 us -> 31.1 us  [call(): pl.pallas_call(kernel, out_shape=outs, in_specs=specs, out_specs=[pl.Bloc...]
where the time goes in v3:
time: 164 us
  waiting for transfers between devices  65.4 us (40%)
  starting transfers between devices  43.4 us (26%)
  Pallas kernels  31.1 us (19%)
  other arithmetic  21.8 us (13%)
    pallas_call x6, Pallas kernels, call(): pl.pallas_call(kernel, out_shape=outs, in_specs=specs, out_specs=[pl.Bloc...  31.1 us
    ppermute x4, waiting for transfers between devices, from_before(): lax.ppermute(value, axis, [(i, (i + 1) % count) for i in range(count)])  30.1 us
    all_to_all x2, starting transfers between devices, body(): lax.all_to_all(spectrum, axes, split_axis=0, concat_axis=0, tiled=True)  25.5 us
    all_to_all x2, waiting for transfers between devices, body(): lax.all_to_all(spectrum, axes, split_axis=0, concat_axis=0, tiled=True)  23.1 us
    convert_element_type x3, other arithmetic, tripled(): high = high.astype(BF16)  14 us
    ppermute x4, waiting for transfers between devices, from_after(): lax.ppermute(value, axis, [((i + 1) % count, i) for i in range(count)])  11 us
    ppermute x4, starting transfers between devices, from_before(): lax.ppermute(value, axis, [(i, (i + 1) % count) for i in range(count)])  9.69 us
    ppermute x1, starting transfers between devices, body(): inflow = lax.ppermute(inflow, 'grp', [(0, 1)])  4.97 us
  transfers between devices with their start and end apart: 11, of which 10 were waited for; matrix products, arithmetic and copies ran while one was open for 14% of the time, Pallas kernels for 0%

profile of v3, /device:TPU:31, one launch (start us, length us, event | category | flops | bytes accessed | tf_op | source)
XLA Modules:
  0.0 163.9 jit_solution(21637741560406612)
XLA Ops:
  0.6 3.6 %shard_map.50 = f32[3072,128]{1,0:T(8,128)} custom-call(f32[3,8,64,256]{3,2,1,0:T(8,128)} %bitcast.7, bf16[2,256,256]{2,1,0:T(8,128)(2,1)} %constant.213.clone.table_any), custom_call_target="tpu_custom_call" | custom-call | tf_op jit(solution)/shard_map/pallas_call | solution.py:518
  4.3 13.3 %all-to-all-start = ((f32[128,24,128]{2,1,0:T(8,128)}), f32[128,24,128]{2,1,0:T(8,128)}, u32[]{:S(2)}, u32[]{:S(2)}) async-start(f32[128,24,128]{2,1,0:T(8,128)} %bitcast.10), calls=%async_computation | async-start | bytes 3145728 | tf_op jit(solution)/shard_map/all_to_all | solution.py:629
  17.5 1.1 fusion.49
  18.6 1.5 collective-permute-start.1
  20.1 2.5 %collective-permute-start = (f32[3,8,2,256]{3,2,1,0:T(2,128)S(1)}, f32[3,8,2,256]{3,2,1,0:T(2,128)S(1)}, u32[]{:S(2)}, u32[]{:S(2)}) collective-permute-start(f32[3,8,2,256]{3,2,1,0:T(2,128)S(1)} %get-tuple-element.51), channel_id=1, source_target_pairs={{32,0},{64,32},{96,64},{0,96},{33,1},{65,33},{97,65},{1,97},{34,2}... | collective-permute-start | bytes 147464 | tf_op jit(solution)/shard_map/ppermute | solution.py:601
  22.7 2.5 %reduce-precision_convert_fusion.2 = (bf16[256,512]{1,0:T(8,128)(2,1)S(1)}, bf16[256,512]{1,0:T(8,128)(2,1)S(1)}) fusion(s32[512]{0:T(512)S(1)} %get-tuple-element.63, s32[512]{0:T(512)S(1)} %get-tuple-element.77, pred[512]{0:T(512)(128)(4,1)S(1)} %get-tuple-element.68, s32[256]{0:T(256)S(1)} %get-tuple-element.72, pred[512]{0:T(512)(128)(4,1)S(1)} %get-tuple-element.64), kind=kLoop, calls=%fused_computation.82 | loop fusion | flops 2621440 | bytes 530432 | tf_op jit(solution)/shard_map/convert_element_type | solution.py:77
  25.3 1.0 pad_maximum_fusion.3.y_any
  26.3 0.8 fusion.40.flip_any
  27.1 1.5 reduce-precision_convert_fusion.3
  28.6 10.0 %reduce-precision_convert_fusion = (bf16[512,512]{1,0:T(8,128)(2,1)S(1)}, bf16[512,512]{1,0:T(8,128)(2,1)S(1)}, bf16[512,512]{1,0:T(8,128)(2,1)S(1)}, bf16[512,512]{1,0:T(8,128)(2,1)S(1)}) fusion(pred[512]{0:T(512)(128)(4,1)S(1)} %get-tuple-element.64, s32[512]{0:T(512)S(1)} %get-tuple-element.62, s32[512]{0:T(512)S(1)} %get-tuple-element.79, ...), kind=kLoop, calls=%fused_computation.43 | loop fusion | flops 29622272 | bytes 2116096 | tf_op jit(solution)/shard_map/convert_element_type | solution.py:77
  38.6 1.3 pad_maximum_fusion.2.back_any
  39.9 1.2 pad_maximum_fusion.1.z_any
  41.2 6.0 %collective-permute-done.1 = f32[3,8,2,256]{3,2,1,0:T(2,128)S(1)} collective-permute-done((f32[3,8,2,256]{3,2,1,0:T(2,128)S(1)}, f32[3,8,2,256]{3,2,1,0:T(2,128)S(1)}, u32[]{:S(2)}, u32[]{:S(2)}) %collective-permute-start.1) | collective-permute-done | bytes 49184 | tf_op jit(solution)/shard_map/ppermute | solution.py:596
  47.2 0.0 collective-permute-done
  47.2 1.6 fusion
  48.8 0.0 copy-start.1
  48.8 6.6 %all-to-all-done.in_any = f32[128,24,128]{2,1,0:T(8,128)} async-done(((f32[128,24,128]{2,1,0:T(8,128)}), f32[128,24,128]{2,1,0:T(8,128)}, u32[]{:S(2)}, u32[]{:S(2)}) %all-to-all-start) | async-done | bytes 1572896 | tf_op jit(solution)/shard_map/all_to_all | solution.py:629
  55.4 10.6 %shard_map.51 = f32[128,24,128]{2,1,0:T(8,128)} custom-call(s32[1]{0:T(128)} %bitcast.2.owner_ref, f32[128,24,128]{2,1,0:T(8,128)} %all-to-all-done.in_any, bf16[512,1536]{1,0:T(8,128)(2,1)} %pad_maximum_fusion.1.z_any, bf16[768,512]{1,0:T(8,128)(2,1)} %pad_maximum_fusion.3.y_any, bf16[512,1536]{1,0:T(8,128)(2,1)} %pad_maximum_fusion.2.back_any, ...), custom_call_target="tpu_custom_call" | custom-call | tf_op jit(solution)/shard_map/pallas_call | solution.py:518
  66.0 12.3 %all-to-all-start.1 = ((f32[128,24,128]{2,1,0:T(8,128)}), f32[128,24,128]{2,1,0:T(8,128)}, u32[]{:S(2)}, u32[]{:S(2)}) async-start(f32[128,24,128]{2,1,0:T(8,128)} %shard_map.51), calls=%async_computation.1 | async-start | bytes 3145728 | tf_op jit(solution)/shard_map/all_to_all | solution.py:637
  78.3 0.0 copy-done.1
  78.3 0.1 fusion.48
  78.3 0.9 collective-permute-start.2
  79.3 0.0 copy-start
  79.3 0.0 collective-permute-start.3
  79.3 14.0 %collective-permute-done.2 = f32[3,2,72,256]{3,2,1,0:T(8,128)S(1)} collective-permute-done((f32[3,2,72,256]{3,2,1,0:T(8,128)S(1)}, f32[3,2,72,256]{3,2,1,0:T(8,128)S(1)}, u32[]{:S(2)}, u32[]{:S(2)}) %collective-permute-start.2) | collective-permute-done | bytes 442400 | tf_op jit(solution)/shard_map/ppermute | solution.py:596
  93.3 3.4 %collective-permute-done.3 = f32[3,2,72,256]{3,2,1,0:T(8,128)S(1)} collective-permute-done((f32[3,2,72,256]{3,2,1,0:T(8,128)S(1)}, f32[3,2,72,256]{3,2,1,0:T(8,128)S(1)}, u32[]{:S(2)}, u32[]{:S(2)}) %collective-permute-start.3) | collective-permute-done | bytes 442400 | tf_op jit(solution)/shard_map/ppermute | solution.py:601
  96.8 1.7 %pad_maximum_fusion.field_ref = f32[3,12,72,256]{3,2,1,0:T(8,128)S(1)} fusion(f32[3,2,72,256]{3,2,1,0:T(8,128)S(1)} %collective-permute-done.3, f32[3,8,72,256]{3,2,1,0:T(8,128)} %copy-done.1, f32[3,2,72,256]{3,2,1,0:T(8,128)S(1)} %collective-permute-done.2), kind=kLoop, calls=%fused_computation.12 | loop fusion | flops 1327104 | bytes 5308416 | tf_op jit(solution)/shard_map/concatenate | solution.py:614
  98.5 16.5 %all-to-all-done.1 = f32[128,24,128]{2,1,0:T(8,128)} async-done(((f32[128,24,128]{2,1,0:T(8,128)}), f32[128,24,128]{2,1,0:T(8,128)}, u32[]{:S(2)}, u32[]{:S(2)}) %all-to-all-start.1) | async-done | bytes 1572896 | tf_op jit(solution)/shard_map/all_to_all | solution.py:637
  115.0 0.0 copy-done
  115.0 2.4 %shard_map.52 = (f32[3,8,64,256]{3,2,1,0:T(8,128)S(1)}, f32[72,256]{1,0:T(8,128)S(1)}, f32[72,256]{1,0:T(8,128)S(1)}) custom-call(f32[3072,128]{1,0:T(8,128)} %bitcast.4.in_ref, bf16[768,256]{1,0:T(8,128)(2,1)S(1)} %pad_maximum_fusion.4.table_ref, f32[1,3]{1,0:T(1,128)S(1)} %copy-done), custom_call_target="tpu_custom_call" | custom-call | tf_op jit(solution)/shard_map/pallas_call | solution.py:518
  117.4 0.7 collective-permute-start.4
  118.1 0.8 collective-permute-start.5
  118.9 1.7 %collective-permute-done.4.above_ref = f32[72,256]{1,0:T(8,128)S(1)} collective-permute-done((f32[72,256]{1,0:T(8,128)S(1)}, f32[72,256]{1,0:T(8,128)S(1)}, u32[]{:S(2)}, u32[]{:S(2)}) %collective-permute-start.4) | collective-permute-done | bytes 73760 | tf_op jit(solution)/shard_map/ppermute | solution.py:601
  120.7 2.4 %collective-permute-done.5.below_ref = f32[72,256]{1,0:T(8,128)S(1)} collective-permute-done((f32[72,256]{1,0:T(8,128)S(1)}, f32[72,256]{1,0:T(8,128)S(1)}, u32[]{:S(2)}, u32[]{:S(2)}) %collective-permute-start.5) | collective-permute-done | bytes 73760 | tf_op jit(solution)/shard_map/ppermute | solution.py:596
  123.1 0.1 shard_map.53
  123.3 6.4 %collective-permute-start.6 = (f32[3,3,72,256]{3,2,1,0:T(8,128)S(1)}, f32[3,3,72,256]{3,2,1,0:T(8,128)S(1)}, u32[]{:S(2)}, u32[]{:S(2)}) collective-permute-start(f32[3,3,72,256]{3,2,1,0:T(8,128)S(1)} %get-tuple-element.43), channel_id=1, source_target_pairs={{0,1},{1,2},{2,3},{3,4},{4,5},{5,6},{6,7},{7,8},{8,9},{9,10},{10,1... | collective-permute-start | bytes 1990664 | tf_op jit(solution)/shard_map/ppermute | solution.py:596
  129.7 0.0 collective-permute-start.7
  129.7 7.6 %collective-permute-done.6.low_ref = f32[3,3,72,256]{3,2,1,0:T(8,128)S(1)} collective-permute-done((f32[3,3,72,256]{3,2,1,0:T(8,128)S(1)}, f32[3,3,72,256]{3,2,1,0:T(8,128)S(1)}, u32[]{:S(2)}, u32[]{:S(2)}) %collective-permute-start.6) | collective-permute-done | bytes 663584 | tf_op jit(solution)/shard_map/ppermute | solution.py:596
  137.3 5.8 %collective-permute-done.7.high_ref = f32[3,3,72,256]{3,2,1,0:T(8,128)S(1)} collective-permute-done((f32[3,3,72,256]{3,2,1,0:T(8,128)S(1)}, f32[3,3,72,256]{3,2,1,0:T(8,128)S(1)}, u32[]{:S(2)}, u32[]{:S(2)}) %collective-permute-start.7) | collective-permute-done | bytes 663584 | tf_op jit(solution)/shard_map/ppermute | solution.py:601
  143.1 1.1 shard_map.54
  144.3 5.0 %collective-permute-start.8 = (f32[112,128]{1,0:T(8,128)S(1)}, f32[112,128]{1,0:T(8,128)S(1)}, u32[]{:S(2)}, u32[]{:S(2)}) collective-permute-start(f32[112,128]{1,0:T(8,128)S(1)} %shard_map.54), channel_id=1, source_target_pairs={{0,128},{1,129},{2,130},{3,131},{4,132},{5,133},{6,134},{7,135},{8... | collective-permute-start | bytes 172040 | tf_op jit(solution)/shard_map/ppermute | solution.py:646
  149.2 1.2 collective-permute-done.8.inflow_ref
  150.5 13.2 %shard_map.55 = (f32[3,8,64,256]{3,2,1,0:T(8,128)}, f32[3,8,64,256]{3,2,1,0:T(8,128)}) custom-call(s32[1]{0:T(128)} %bitcast.1.wake_ref, f32[3,8,64,256]{3,2,1,0:T(8,128)S(1)} %get-tuple-element.39.speed_ref, f32[3,8,8,256]{3,2,1,0:T(8,128)S(1)} %get-tuple-element.42.tail_ref, f32[3,3,72,256]{3,2,1,0:T(8,128)S(1)} %collective-permute-done.6.low_ref, ...), custom_call_target="tpu_custom_call" | custom-call | tf_op jit(solution)/shard_map/pallas_call | solution.py:518
  (13 shorter events, 0.1 us)
Async XLA Ops:
  4.3 51.1 %all-to-all-start = ((f32[128,24,128]{2,1,0:T(8,128)}), f32[128,24,128]{2,1,0:T(8,128)}, u32[]{:S(2)}, u32[]{:S(2)}) async-start(f32[128,24,128]{2,1,0:T(8,128)} %bitcast.10), calls=%async_computation | async-start | bytes 3145728 | tf_op jit(solution)/shard_map/all_to_all | solution.py:629
  18.6 28.6 %collective-permute-start.1 = (f32[3,8,2,256]{3,2,1,0:T(2,128)S(1)}, f32[3,8,2,256]{3,2,1,0:T(2,128)S(1)}, u32[]{:S(2)}, u32[]{:S(2)}) collective-permute-start(f32[3,8,2,256]{3,2,1,0:T(2,128)S(1)} %get-tuple-element.50), channel_id=1, source_target_pairs={{0,32},{32,64},{64,96},{96,0},{1,33},{33,65},{65,97},{97,1},{2,34}... | collective-permute-start | bytes 147464 | tf_op jit(solution)/shard_map/ppermute | solution.py:596
  20.1 27.1 %collective-permute-start = (f32[3,8,2,256]{3,2,1,0:T(2,128)S(1)}, f32[3,8,2,256]{3,2,1,0:T(2,128)S(1)}, u32[]{:S(2)}, u32[]{:S(2)}) collective-permute-start(f32[3,8,2,256]{3,2,1,0:T(2,128)S(1)} %get-tuple-element.51), channel_id=1, source_target_pairs={{32,0},{64,32},{96,64},{0,96},{33,1},{65,33},{97,65},{1,97},{34,2}... | collective-permute-start | bytes 147464 | tf_op jit(solution)/shard_map/ppermute | solution.py:601
  48.8 29.5 %copy-start.1 = (f32[3,8,72,256]{3,2,1,0:T(8,128)}, f32[3,8,72,256]{3,2,1,0:T(8,128)S(1)}, u32[]{:S(2)}) copy-start(f32[3,8,72,256]{3,2,1,0:T(8,128)S(1)} %fusion) | copy-start | bytes 5308420
  66.0 49.0 %all-to-all-start.1 = ((f32[128,24,128]{2,1,0:T(8,128)}), f32[128,24,128]{2,1,0:T(8,128)}, u32[]{:S(2)}, u32[]{:S(2)}) async-start(f32[128,24,128]{2,1,0:T(8,128)} %shard_map.51), calls=%async_computation.1 | async-start | bytes 3145728 | tf_op jit(solution)/shard_map/all_to_all | solution.py:637
  78.3 15.0 %collective-permute-start.2 = (f32[3,2,72,256]{3,2,1,0:T(8,128)S(1)}, f32[3,2,72,256]{3,2,1,0:T(8,128)S(1)}, u32[]{:S(2)}, u32[]{:S(2)}) collective-permute-start(f32[3,2,72,256]{3,2,1,0:T(8,128)S(1)} %get-tuple-element.48), channel_id=1, source_target_pairs={{0,1},{1,2},{2,3},{3,4},{4,5},{5,6},{6,7},{7,8},{8,9},{9,10},{10,1... | collective-permute-start | bytes 1327112 | tf_op jit(solution)/shard_map/ppermute | solution.py:596
  79.3 35.7 %copy-start = (f32[1,3]{1,0:T(1,128)S(1)}, f32[1,3]{1,0:T(1,128)}, u32[]{:S(2)}) copy-start(f32[1,3]{1,0:T(1,128)} %drift_ref.1) | copy-start | bytes 40
  79.3 17.5 %collective-permute-start.3 = (f32[3,2,72,256]{3,2,1,0:T(8,128)S(1)}, f32[3,2,72,256]{3,2,1,0:T(8,128)S(1)}, u32[]{:S(2)}, u32[]{:S(2)}) collective-permute-start(f32[3,2,72,256]{3,2,1,0:T(8,128)S(1)} %get-tuple-element.49), channel_id=1, source_target_pairs={{1,0},{2,1},{3,2},{4,3},{5,4},{6,5},{7,6},{8,7},{9,8},{10,9},{11,1... | collective-permute-start | bytes 1327112 | tf_op jit(solution)/shard_map/ppermute | solution.py:601
  117.4 3.3 %collective-permute-start.4 = (f32[72,256]{1,0:T(8,128)S(1)}, f32[72,256]{1,0:T(8,128)S(1)}, u32[]{:S(2)}, u32[]{:S(2)}) collective-permute-start(f32[72,256]{1,0:T(8,128)S(1)} %get-tuple-element.40), channel_id=1, source_target_pairs={{32,0},{64,32},{96,64},{0,96},{33,1},{65,33},{97,65},{1,97},{34,2}... | collective-permute-start | bytes 221192 | tf_op jit(solution)/shard_map/ppermute | solution.py:601
  118.1 5.0 %collective-permute-start.5 = (f32[72,256]{1,0:T(8,128)S(1)}, f32[72,256]{1,0:T(8,128)S(1)}, u32[]{:S(2)}, u32[]{:S(2)}) collective-permute-start(f32[72,256]{1,0:T(8,128)S(1)} %get-tuple-element.41), channel_id=1, source_target_pairs={{0,32},{32,64},{64,96},{96,0},{1,33},{33,65},{65,97},{97,1},{2,34}... | collective-permute-start | bytes 221192 | tf_op jit(solution)/shard_map/ppermute | solution.py:596
  123.3 14.1 %collective-permute-start.6 = (f32[3,3,72,256]{3,2,1,0:T(8,128)S(1)}, f32[3,3,72,256]{3,2,1,0:T(8,128)S(1)}, u32[]{:S(2)}, u32[]{:S(2)}) collective-permute-start(f32[3,3,72,256]{3,2,1,0:T(8,128)S(1)} %get-tuple-element.43), channel_id=1, source_target_pairs={{0,1},{1,2},{2,3},{3,4},{4,5},{5,6},{6,7},{7,8},{8,9},{9,10},{10,1... | collective-permute-start | bytes 1990664 | tf_op jit(solution)/shard_map/ppermute | solution.py:596
  129.7 13.4 %collective-permute-start.7 = (f32[3,3,72,256]{3,2,1,0:T(8,128)S(1)}, f32[3,3,72,256]{3,2,1,0:T(8,128)S(1)}, u32[]{:S(2)}, u32[]{:S(2)}) collective-permute-start(f32[3,3,72,256]{3,2,1,0:T(8,128)S(1)} %get-tuple-element.44), channel_id=1, source_target_pairs={{1,0},{2,1},{3,2},{4,3},{5,4},{6,5},{7,6},{8,7},{9,8},{10,9},{11,1... | collective-permute-start | bytes 1990664 | tf_op jit(solution)/shard_map/ppermute | solution.py:601
  144.3 6.2 %collective-permute-start.8 = (f32[112,128]{1,0:T(8,128)S(1)}, f32[112,128]{1,0:T(8,128)S(1)}, u32[]{:S(2)}, u32[]{:S(2)}) collective-permute-start(f32[112,128]{1,0:T(8,128)S(1)} %shard_map.54), channel_id=1, source_target_pairs={{0,128},{1,129},{2,130},{3,131},{4,132},{5,133},{6,134},{7,135},{8... | collective-permute-start | bytes 172040 | tf_op jit(solution)/shard_map/ppermute | solution.py:646

commit v4 on v3

--- a/solution.py
+++ b/solution.py
@@ -217,7 +217,7 @@
 
 
 def streamwise_backward(
-    in_ref, table_ref, drift_ref, out_ref, low_ref, high_ref
+    in_ref, table_ref, drift_ref, out_ref, low_ref, high_ref, up_ref, down_ref
 ):
     comps, local_z, local_y, count = out_ref.shape
 
@@ -230,7 +230,10 @@
             parts.append(jnp.concatenate(chunks, 1))
         value = jnp.concatenate(parts, 0).T
         result = right_product(value, table_ref[...]) + drift_ref[0, c]
-        out_ref[c] = result.reshape(local_z, local_y, count)
+        result = result.reshape(local_z, local_y, count)
+        out_ref[c] = result
+        up_ref[c] = result[local_z - RIM :]
+        down_ref[c] = result[:RIM]
     for c in range(comps):
         for z in range(local_z):
             row = (c * local_z + z) * RIM
@@ -238,18 +241,16 @@
             high_ref[row : row + RIM, :] = out_ref[c, z, local_y - RIM : local_y, :]
 
 
-def edge_kernel(speed_ref, above_ref, below_ref, tail_ref, up_ref, down_ref):
-    comps, local_z, local_y, count = speed_ref.shape
+def edge_kernel(above_ref, below_ref, tail_ref, up_ref, down_ref):
+    comps, local_z, _, count = tail_ref.shape
     for c in range(comps):
         for z in range(local_z):
             row = (c * local_z + z) * RIM
             tail_ref[c, z, 0:RIM, :] = above_ref[row : row + RIM, :]
             tail_ref[c, z, RIM : 8 - RIM, :] = jnp.zeros((8 - 2 * RIM, count), F32)
             tail_ref[c, z, 8 - RIM : 8, :] = below_ref[row : row + RIM, :]
-        for target, first in ((up_ref, local_z - RIM), (down_ref, 0)):
-            for z in range(RIM):
-                target[c, z, 0:local_y, :] = speed_ref[c, first + z]
-                target[c, z, local_y : local_y + 8, :] = tail_ref[c, first + z]
+        up_ref[c] = tail_ref[c, local_z - RIM :]
+        down_ref[c] = tail_ref[c, :RIM]
 
 
 def weights(shift, small=False):
@@ -283,7 +284,10 @@
     return pltpu.roll(value, steps % value.shape[1], 1)
 
 
-def inflow_kernel(wake_ref, speed_ref, tail_ref, low_ref, high_ref, field_ref, out_ref, line_ref):
+def inflow_kernel(
+    wake_ref, speed_ref, tail_ref, low_ref, low_tail_ref, high_ref, high_tail_ref, field_ref,
+    out_ref, line_ref,
+):
     planes, local_z = field_ref.shape[1], speed_ref.shape[1]
     lane = lax.broadcasted_iota(jnp.int32, (72, 128), 1)
 
@@ -295,17 +299,15 @@
             base = 24 * (q % 5)
             for c in range(3):
                 if q < RIM:
-                    first, last = low_ref[c, q, :, :128], low_ref[c, q, :, 128:]
+                    own, end, z = low_ref, low_tail_ref, q
                 elif q < RIM + local_z:
-                    z = q - RIM
-                    pieces = [
-                        jnp.concatenate([speed_ref[c, z, :, lanes], tail_ref[c, z, :, lanes]], 0)
-                        for lanes in (slice(0, 128), slice(128, 256))
-                    ]
-                    first, last = pieces
+                    own, end, z = speed_ref, tail_ref, q - RIM
                 else:
-                    z = q - RIM - local_z
-                    first, last = high_ref[c, z, :, :128], high_ref[c, z, :, 128:]
+                    own, end, z = high_ref, high_tail_ref, q - RIM - local_z
+                first, last = [
+                    jnp.concatenate([own[c, z, :, lanes], end[c, z, :, lanes]], 0)
+                    for lanes in (slice(0, 128), slice(128, 256))
+                ]
                 at = base + 4 * c
                 here = (lane >= at) & (lane < at + 4)
                 ends = jnp.where(lane < 64, first, last)
@@ -353,20 +355,20 @@
             out_ref[first : first + planes, :] = rows[2][:planes]
 
 
-def fill_speed(speed_ref, tail_ref, low_ref, high_ref, all_ref):
+def fill_speed(speed_ref, tail_ref, low_ref, low_tail_ref, high_ref, high_tail_ref, all_ref):
     local_z = speed_ref.shape[1]
     most = jnp.zeros((8, 128), F32)
     for c in range(3):
         for t in range(2):
             lanes = slice(128 * t, 128 * t + 128)
-            for own, end, row, first in (
-                (low_ref, low_ref, 64, 0),
-                (speed_ref, tail_ref, 0, RIM),
-                (high_ref, high_ref, 64, RIM + local_z),
+            for own, end, first in (
+                (low_ref, low_tail_ref, 0),
+                (speed_ref, tail_ref, RIM),
+                (high_ref, high_tail_ref, RIM + local_z),
             ):
                 planes = slice(first, first + own.shape[1])
                 body = own[c, :, 0:64, lanes]
-                tail = end[c, :, row : row + 8, lanes]
+                tail = end[c, :, :, lanes]
                 all_ref[c, planes, t, 8:72, :] = body
                 all_ref[c, planes, t, 0:8, :] = tail
                 all_ref[c, planes, t, 72:80, :] = tail
@@ -377,7 +379,8 @@
 
 
 def wake_kernel(
-    wake_ref, speed_ref, tail_ref, low_ref, high_ref, field_ref, inflow_ref, out_ref, speed_any,
+    wake_ref, speed_ref, tail_ref, low_ref, low_tail_ref, high_ref, high_tail_ref, field_ref,
+    inflow_ref, out_ref, speed_any,
     all_ref, column_ref, moved_ref, across_ref, lateral_ref, upward_ref, sem,
 ):
     copy = pltpu.make_async_copy(speed_ref, speed_any, sem)
@@ -391,7 +394,9 @@
     leaving_lane = is_wake & (lane == 127)
     inflow_lanes = is_wake & (lane < 2)
     crossing = {o: is_wake & (lane >= 128 - o if o > 0 else lane < -o) for o in (-2, -1, 1, 2)}
-    most = fill_speed(speed_ref, tail_ref, low_ref, high_ref, all_ref)
+    most = fill_speed(
+        speed_ref, tail_ref, low_ref, low_tail_ref, high_ref, high_tail_ref, all_ref
+    )
     missing = 128 - inflow_ref.shape[0]
     column_ref[...] = jnp.concatenate([inflow_ref[...], jnp.zeros((missing, 128), F32)], 0).T
     is_small = TIME_STEP * most < 0.999
@@ -556,26 +561,27 @@
 
 def backward_lines(spectrum, drift, table, shape):
     edge = (shape[0] * shape[1] * RIM, shape[3])
-    shapes = [shape, edge, edge]
+    planes = (shape[0], RIM, *shape[2:])
+    shapes = [shape, edge, edge, planes, planes]
     return call(streamwise_backward, shapes, (spectrum, table, drift), smem=(2,))
 
 
-def with_edges(speed, above, below):
-    comps, local_z, local_y, count = speed.shape
-    send = (comps, RIM, local_y + 8, count)
-    shapes = [(comps, local_z, 8, count), send, send]
-    return call(edge_kernel, shapes, (speed, above, below))
-
-
-def inflow_columns(wake, speed, tail, low, high, field):
-    args = (wake, speed, tail, low, high, field)
-    scratch = [pltpu.VMEM((24 * (field.shape[1] + 6), 128), F32)]
-    shape = (9 * field.shape[1] + 4, 128)
-    return call(inflow_kernel, shape, args, smem=(0,), scratch=scratch)
-
-
-def wake_step(wake, speed, tail, low, high, field, inflow):
-    comps, local_z, local_y, count = speed.shape
+def edges(above, below, shape):
+    comps, local_z, _, count = shape
+    send = (comps, RIM, 8, count)
+    return call(edge_kernel, [(comps, local_z, 8, count), send, send], (above, below))
+
+
+def inflow_columns(wake, *arrays):
+    planes = arrays[-1].shape[1]
+    scratch = [pltpu.VMEM((24 * (planes + 6), 128), F32)]
+    args = (wake, *arrays)
+    return call(inflow_kernel, (9 * planes + 4, 128), args, smem=(0,), scratch=scratch)
+
+
+def wake_step(wake, *arrays):
+    shape = arrays[0].shape
+    comps, local_z, local_y, count = shape
     lanes, planes = count // 128, local_z + 4
     scratch = [
         pltpu.VMEM((comps, planes + 2, lanes, local_y + 24, 128), F32),
@@ -586,9 +592,8 @@
         pltpu.VMEM((5, planes, lanes, local_y, 128), F32),
         pltpu.SemaphoreType.DMA,
     ]
-    args = (wake, speed, tail, low, high, field, inflow)
-    shapes = [speed.shape, speed.shape]
-    return call(wake_kernel, shapes, args, smem=(0,), far_out=(1,), scratch=scratch)
+    args = (wake, *arrays)
+    return call(wake_kernel, [shape, shape], args, smem=(0,), far_out=(1,), scratch=scratch)
 
 
 def from_before(value, axis):
@@ -638,13 +643,14 @@
     wide = wider_planes(wide)
     spectrum, wide = lax.optimization_barrier((spectrum, wide))
     spectrum = spectrum.reshape(groups * 24, 128)
-    speed, first, last = backward_lines(spectrum, wind, streamwise, field.shape)
+    speed, first, last, up, down = backward_lines(spectrum, wind, streamwise, field.shape)
     above, below = from_after(first, "gy"), from_before(last, "gy")
-    tail, up, down = with_edges(speed, above, below)
     low, high = from_before(up, "gz"), from_after(down, "gz")
-    inflow = inflow_columns(wake, speed, tail, low, high, wide)
-    inflow = lax.ppermute(inflow, "grp", [(0, 1)])
-    result, velocity = wake_step(wake, speed, tail, low, high, wide, inflow)
+    tail, up_tail, down_tail = edges(above, below, speed.shape)
+    low_tail, high_tail = from_before(up_tail, "gz"), from_after(down_tail, "gz")
+    arrays = (speed, tail, low, low_tail, high, high_tail, wide)
+    inflow = lax.ppermute(inflow_columns(wake, *arrays), "grp", [(0, 1)])
+    result, velocity = wake_step(wake, *arrays, inflow)
     return (result[None], velocity[None])
 
 

time: 164 us -> 163 us (level)
  waiting for transfers between devices: 65.4 us -> 59.2 us
  starting transfers between devices: 43.4 us -> 48.4 us
    ppermute x4 -> x5, waiting for transfers between devices: 30.1 us -> 23.7 us  [from_before(): lax.ppermute(value, axis, [(i, (i + 1) % count) for i in range(count)])]
    ppermute x4 -> x5, starting transfers between devices: 9.69 us -> 14.6 us  [from_before(): lax.ppermute(value, axis, [(i, (i + 1) % count) for i in range(count)])]
    ppermute x4 -> x5, waiting for transfers between devices: 11 us -> 11.1 us  [from_after(): lax.ppermute(value, axis, [((i + 1) % count, i) for i in range(count)])]
  transfers between devices with their start and end apart: 11 -> 13, of which waited for: 10 -> 10; matrix products, arithmetic and copies ran while one was open for 14% -> 14% of each run, Pallas kernels for 0% -> 0%
where the time goes in v4:
time: 163 us
  waiting for transfers between devices  59.2 us (36%)
  starting transfers between devices  48.4 us (30%)
  Pallas kernels  31.3 us (19%)
  other arithmetic  21.8 us (13%)
    pallas_call x6, Pallas kernels, call(): pl.pallas_call(kernel, out_shape=outs, in_specs=specs, out_specs=[pl.Bloc...  31.3 us
    all_to_all x2, starting transfers between devices, body(): lax.all_to_all(spectrum, axes, split_axis=0, concat_axis=0, tiled=True)  25.5 us
    ppermute x5, waiting for transfers between devices, from_before(): lax.ppermute(value, axis, [(i, (i + 1) % count) for i in range(count)])  23.7 us
    all_to_all x2, waiting for transfers between devices, body(): lax.all_to_all(spectrum, axes, split_axis=0, concat_axis=0, tiled=True)  23.1 us
    ppermute x5, starting transfers between devices, from_before(): lax.ppermute(value, axis, [(i, (i + 1) % count) for i in range(count)])  14.6 us
    convert_element_type x3, other arithmetic, tripled(): high = high.astype(BF16)  14 us
    ppermute x5, waiting for transfers between devices, from_after(): lax.ppermute(value, axis, [((i + 1) % count, i) for i in range(count)])  11.1 us
    ppermute x1, starting transfers between devices, body(): inflow = lax.ppermute(inflow_columns(wake, *arrays), 'grp', [(0, 1)])  4.99 us
  transfers between devices with their start and end apart: 13, of which 10 were waited for; matrix products, arithmetic and copies ran while one was open for 14% of the time, Pallas kernels for 0%

profile of v4, /device:TPU:31, one launch (start us, length us, event | category | flops | bytes accessed | tf_op | source)
XLA Modules:
  0.0 162.9 jit_solution(15953560352022512652)
XLA Ops:
  0.6 3.6 %shard_map.50 = f32[3072,128]{1,0:T(8,128)} custom-call(f32[3,8,64,256]{3,2,1,0:T(8,128)} %bitcast.7, bf16[2,256,256]{2,1,0:T(8,128)(2,1)} %constant.213.clone.table_any), custom_call_target="tpu_custom_call" | custom-call | tf_op jit(solution)/shard_map/pallas_call | solution.py:523
  4.3 13.3 %all-to-all-start = ((f32[128,24,128]{2,1,0:T(8,128)}), f32[128,24,128]{2,1,0:T(8,128)}, u32[]{:S(2)}, u32[]{:S(2)}) async-start(f32[128,24,128]{2,1,0:T(8,128)} %bitcast.10), calls=%async_computation | async-start | bytes 3145728 | tf_op jit(solution)/shard_map/all_to_all | solution.py:634
  17.5 1.1 fusion.49
  18.6 1.5 collective-permute-start.1
  20.1 2.5 %collective-permute-start = (f32[3,8,2,256]{3,2,1,0:T(2,128)S(1)}, f32[3,8,2,256]{3,2,1,0:T(2,128)S(1)}, u32[]{:S(2)}, u32[]{:S(2)}) collective-permute-start(f32[3,8,2,256]{3,2,1,0:T(2,128)S(1)} %get-tuple-element.55), channel_id=1, source_target_pairs={{32,0},{64,32},{96,64},{0,96},{33,1},{65,33},{97,65},{1,97},{34,2}... | collective-permute-start | bytes 147464 | tf_op jit(solution)/shard_map/ppermute | solution.py:606
  22.7 2.5 %reduce-precision_convert_fusion.2 = (bf16[256,512]{1,0:T(8,128)(2,1)S(1)}, bf16[256,512]{1,0:T(8,128)(2,1)S(1)}) fusion(s32[512]{0:T(512)S(1)} %get-tuple-element.67, s32[512]{0:T(512)S(1)} %get-tuple-element.81, pred[512]{0:T(512)(128)(4,1)S(1)} %get-tuple-element.72, s32[256]{0:T(256)S(1)} %get-tuple-element.76, pred[512]{0:T(512)(128)(4,1)S(1)} %get-tuple-element.68), kind=kLoop, calls=%fused_computation.82 | loop fusion | flops 2621440 | bytes 530432 | tf_op jit(solution)/shard_map/convert_element_type | solution.py:77
  25.3 1.0 pad_maximum_fusion.3.y_any
  26.2 0.8 fusion.40.flip_any
  27.1 1.5 reduce-precision_convert_fusion.3
  28.6 10.0 %reduce-precision_convert_fusion = (bf16[512,512]{1,0:T(8,128)(2,1)S(1)}, bf16[512,512]{1,0:T(8,128)(2,1)S(1)}, bf16[512,512]{1,0:T(8,128)(2,1)S(1)}, bf16[512,512]{1,0:T(8,128)(2,1)S(1)}) fusion(pred[512]{0:T(512)(128)(4,1)S(1)} %get-tuple-element.68, s32[512]{0:T(512)S(1)} %get-tuple-element.66, s32[512]{0:T(512)S(1)} %get-tuple-element.83, ...), kind=kLoop, calls=%fused_computation.43 | loop fusion | flops 29622272 | bytes 2116096 | tf_op jit(solution)/shard_map/convert_element_type | solution.py:77
  38.6 1.3 pad_maximum_fusion.2.back_any
  39.9 1.2 pad_maximum_fusion.1.z_any
  41.2 6.0 %collective-permute-done.1 = f32[3,8,2,256]{3,2,1,0:T(2,128)S(1)} collective-permute-done((f32[3,8,2,256]{3,2,1,0:T(2,128)S(1)}, f32[3,8,2,256]{3,2,1,0:T(2,128)S(1)}, u32[]{:S(2)}, u32[]{:S(2)}) %collective-permute-start.1) | collective-permute-done | bytes 49184 | tf_op jit(solution)/shard_map/ppermute | solution.py:601
  47.2 0.0 collective-permute-done
  47.2 1.6 fusion
  48.8 0.0 copy-start.1
  48.8 6.6 %all-to-all-done.in_any = f32[128,24,128]{2,1,0:T(8,128)} async-done(((f32[128,24,128]{2,1,0:T(8,128)}), f32[128,24,128]{2,1,0:T(8,128)}, u32[]{:S(2)}, u32[]{:S(2)}) %all-to-all-start) | async-done | bytes 1572896 | tf_op jit(solution)/shard_map/all_to_all | solution.py:634
  55.4 10.6 %shard_map.51 = f32[128,24,128]{2,1,0:T(8,128)} custom-call(s32[1]{0:T(128)} %bitcast.2.owner_ref, f32[128,24,128]{2,1,0:T(8,128)} %all-to-all-done.in_any, bf16[512,1536]{1,0:T(8,128)(2,1)} %pad_maximum_fusion.1.z_any, bf16[768,512]{1,0:T(8,128)(2,1)} %pad_maximum_fusion.3.y_any, bf16[512,1536]{1,0:T(8,128)(2,1)} %pad_maximum_fusion.2.back_any, ...), custom_call_target="tpu_custom_call" | custom-call | tf_op jit(solution)/shard_map/pallas_call | solution.py:523
  66.0 12.3 %all-to-all-start.1 = ((f32[128,24,128]{2,1,0:T(8,128)}), f32[128,24,128]{2,1,0:T(8,128)}, u32[]{:S(2)}, u32[]{:S(2)}) async-start(f32[128,24,128]{2,1,0:T(8,128)} %shard_map.51), calls=%async_computation.1 | async-start | bytes 3145728 | tf_op jit(solution)/shard_map/all_to_all | solution.py:642
  78.3 0.0 copy-done.1
  78.3 0.1 fusion.48
  78.3 0.9 collective-permute-start.2
  79.3 0.0 copy-start
  79.3 0.0 collective-permute-start.3
  79.3 14.0 %collective-permute-done.2 = f32[3,2,72,256]{3,2,1,0:T(8,128)S(1)} collective-permute-done((f32[3,2,72,256]{3,2,1,0:T(8,128)S(1)}, f32[3,2,72,256]{3,2,1,0:T(8,128)S(1)}, u32[]{:S(2)}, u32[]{:S(2)}) %collective-permute-start.2) | collective-permute-done | bytes 442400 | tf_op jit(solution)/shard_map/ppermute | solution.py:601
  93.3 3.4 %collective-permute-done.3 = f32[3,2,72,256]{3,2,1,0:T(8,128)S(1)} collective-permute-done((f32[3,2,72,256]{3,2,1,0:T(8,128)S(1)}, f32[3,2,72,256]{3,2,1,0:T(8,128)S(1)}, u32[]{:S(2)}, u32[]{:S(2)}) %collective-permute-start.3) | collective-permute-done | bytes 442400 | tf_op jit(solution)/shard_map/ppermute | solution.py:606
  96.8 1.7 %pad_maximum_fusion.field_ref = f32[3,12,72,256]{3,2,1,0:T(8,128)S(1)} fusion(f32[3,2,72,256]{3,2,1,0:T(8,128)S(1)} %collective-permute-done.3, f32[3,8,72,256]{3,2,1,0:T(8,128)} %copy-done.1, f32[3,2,72,256]{3,2,1,0:T(8,128)S(1)} %collective-permute-done.2), kind=kLoop, calls=%fused_computation.12 | loop fusion | flops 1327104 | bytes 5308416 | tf_op jit(solution)/shard_map/concatenate | solution.py:619
  98.5 16.5 %all-to-all-done.1 = f32[128,24,128]{2,1,0:T(8,128)} async-done(((f32[128,24,128]{2,1,0:T(8,128)}), f32[128,24,128]{2,1,0:T(8,128)}, u32[]{:S(2)}, u32[]{:S(2)}) %all-to-all-start.1) | async-done | bytes 1572896 | tf_op jit(solution)/shard_map/all_to_all | solution.py:642
  115.0 0.0 copy-done
  115.0 2.4 %shard_map.52 = (f32[3,8,64,256]{3,2,1,0:T(8,128)S(1)}, f32[72,256]{1,0:T(8,128)S(1)}, f32[72,256]{1,0:T(8,128)S(1)}, f32[3,3,64,256]{3,2,1,0:T(8,128)S(1)}, f32[3,3,64,256]{3,2,1,0:T(8,128)S(1)}) custom-call(f32[3072,128]{1,0:T(8,128)} %bitcast.4.in_ref, bf16[768,256]{1,0:T(8,128)(2,1)S(1)} %pad_maximum_fusion.4.table_ref, f32[1,3]{1,0:T(1,128)S(1)} %copy-done), custom_call_target="tpu_custom_call" | custom-call | tf_op jit(solution)/shard_map/pallas_call | solution.py:523
  117.4 4.9 %collective-permute-start.6 = (f32[3,3,64,256]{3,2,1,0:T(8,128)S(1)}, f32[3,3,64,256]{3,2,1,0:T(8,128)S(1)}, u32[]{:S(2)}, u32[]{:S(2)}) collective-permute-start(f32[3,3,64,256]{3,2,1,0:T(8,128)S(1)} %get-tuple-element.45), channel_id=1, source_target_pairs={{0,1},{1,2},{2,3},{3,4},{4,5},{5,6},{6,7},{7,8},{8,9},{9,10},{10,1... | collective-permute-start | bytes 1769480 | tf_op jit(solution)/shard_map/ppermute | solution.py:601
  122.3 0.0 collective-permute-start.8
  122.3 0.7 collective-permute-start.4
  123.1 0.7 collective-permute-start.5
  123.8 2.0 %collective-permute-done.4.above_ref = f32[72,256]{1,0:T(8,128)S(1)} collective-permute-done((f32[72,256]{1,0:T(8,128)S(1)}, f32[72,256]{1,0:T(8,128)S(1)}, u32[]{:S(2)}, u32[]{:S(2)}) %collective-permute-start.4) | collective-permute-done | bytes 73760 | tf_op jit(solution)/shard_map/ppermute | solution.py:606
  125.8 2.2 %collective-permute-done.5.below_ref = f32[72,256]{1,0:T(8,128)S(1)} collective-permute-done((f32[72,256]{1,0:T(8,128)S(1)}, f32[72,256]{1,0:T(8,128)S(1)}, u32[]{:S(2)}, u32[]{:S(2)}) %collective-permute-start.5) | collective-permute-done | bytes 73760 | tf_op jit(solution)/shard_map/ppermute | solution.py:601
  128.1 0.1 shard_map.53
  128.1 6.6 %collective-permute-start.7 = (f32[3,3,8,256]{3,2,1,0:T(8,128)S(1)}, f32[3,3,8,256]{3,2,1,0:T(8,128)S(1)}, u32[]{:S(2)}, u32[]{:S(2)}) collective-permute-start(f32[3,3,8,256]{3,2,1,0:T(8,128)S(1)} %get-tuple-element.46), channel_id=1, source_target_pairs={{0,1},{1,2},{2,3},{3,4},{4,5},{5,6},{6,7},{7,8},{8,9},{9,10},{10,1... | collective-permute-start | bytes 221192 | tf_op jit(solution)/shard_map/ppermute | solution.py:601
  134.7 0.0 collective-permute-start.9
  134.7 1.4 collective-permute-done.7.low_tail_ref
  136.1 5.7 %collective-permute-done.9.high_tail_ref = f32[3,3,8,256]{3,2,1,0:T(8,128)S(1)} collective-permute-done((f32[3,3,8,256]{3,2,1,0:T(8,128)S(1)}, f32[3,3,8,256]{3,2,1,0:T(8,128)S(1)}, u32[]{:S(2)}, u32[]{:S(2)}) %collective-permute-start.9) | collective-permute-done | bytes 73760 | tf_op jit(solution)/shard_map/ppermute | solution.py:606
  141.8 0.0 collective-permute-done.6.low_ref
  141.8 0.0 collective-permute-done.8.high_ref
  141.8 1.4 shard_map.54
  143.2 5.0 %collective-permute-start.10 = (f32[112,128]{1,0:T(8,128)S(1)}, f32[112,128]{1,0:T(8,128)S(1)}, u32[]{:S(2)}, u32[]{:S(2)}) collective-permute-start(f32[112,128]{1,0:T(8,128)S(1)} %shard_map.54), channel_id=1, source_target_pairs={{0,128},{1,129},{2,130},{3,131},{4,132},{5,133},{6,134},{7,135},{8... | collective-permute-start | bytes 172040 | tf_op jit(solution)/shard_map/ppermute | solution.py:652
  148.2 1.2 collective-permute-done.10.inflow_ref
  149.4 13.2 %shard_map.55 = (f32[3,8,64,256]{3,2,1,0:T(8,128)}, f32[3,8,64,256]{3,2,1,0:T(8,128)}) custom-call(s32[1]{0:T(128)} %bitcast.1.wake_ref, f32[3,8,64,256]{3,2,1,0:T(8,128)S(1)} %get-tuple-element.41.speed_ref, f32[3,8,8,256]{3,2,1,0:T(8,128)S(1)} %get-tuple-element.44.tail_ref, f32[3,3,64,256]{3,2,1,0:T(8,128)S(1)} %collective-permute-done.6.low_ref, ...), custom_call_target="tpu_custom_call" | custom-call | tf_op jit(solution)/shard_map/pallas_call | solution.py:523
  (13 shorter events, 0.1 us)
Async XLA Ops:
  4.3 51.1 %all-to-all-start = ((f32[128,24,128]{2,1,0:T(8,128)}), f32[128,24,128]{2,1,0:T(8,128)}, u32[]{:S(2)}, u32[]{:S(2)}) async-start(f32[128,24,128]{2,1,0:T(8,128)} %bitcast.10), calls=%async_computation | async-start | bytes 3145728 | tf_op jit(solution)/shard_map/all_to_all | solution.py:634
  18.6 28.6 %collective-permute-start.1 = (f32[3,8,2,256]{3,2,1,0:T(2,128)S(1)}, f32[3,8,2,256]{3,2,1,0:T(2,128)S(1)}, u32[]{:S(2)}, u32[]{:S(2)}) collective-permute-start(f32[3,8,2,256]{3,2,1,0:T(2,128)S(1)} %get-tuple-element.54), channel_id=1, source_target_pairs={{0,32},{32,64},{64,96},{96,0},{1,33},{33,65},{65,97},{97,1},{2,34}... | collective-permute-start | bytes 147464 | tf_op jit(solution)/shard_map/ppermute | solution.py:601
  20.1 27.1 %collective-permute-start = (f32[3,8,2,256]{3,2,1,0:T(2,128)S(1)}, f32[3,8,2,256]{3,2,1,0:T(2,128)S(1)}, u32[]{:S(2)}, u32[]{:S(2)}) collective-permute-start(f32[3,8,2,256]{3,2,1,0:T(2,128)S(1)} %get-tuple-element.55), channel_id=1, source_target_pairs={{32,0},{64,32},{96,64},{0,96},{33,1},{65,33},{97,65},{1,97},{34,2}... | collective-permute-start | bytes 147464 | tf_op jit(solution)/shard_map/ppermute | solution.py:606
  48.8 29.5 %copy-start.1 = (f32[3,8,72,256]{3,2,1,0:T(8,128)}, f32[3,8,72,256]{3,2,1,0:T(8,128)S(1)}, u32[]{:S(2)}) copy-start(f32[3,8,72,256]{3,2,1,0:T(8,128)S(1)} %fusion) | copy-start | bytes 5308420
  66.0 49.0 %all-to-all-start.1 = ((f32[128,24,128]{2,1,0:T(8,128)}), f32[128,24,128]{2,1,0:T(8,128)}, u32[]{:S(2)}, u32[]{:S(2)}) async-start(f32[128,24,128]{2,1,0:T(8,128)} %shard_map.51), calls=%async_computation.1 | async-start | bytes 3145728 | tf_op jit(solution)/shard_map/all_to_all | solution.py:642
  78.3 15.0 %collective-permute-start.2 = (f32[3,2,72,256]{3,2,1,0:T(8,128)S(1)}, f32[3,2,72,256]{3,2,1,0:T(8,128)S(1)}, u32[]{:S(2)}, u32[]{:S(2)}) collective-permute-start(f32[3,2,72,256]{3,2,1,0:T(8,128)S(1)} %get-tuple-element.52), channel_id=1, source_target_pairs={{0,1},{1,2},{2,3},{3,4},{4,5},{5,6},{6,7},{7,8},{8,9},{9,10},{10,1... | collective-permute-start | bytes 1327112 | tf_op jit(solution)/shard_map/ppermute | solution.py:601
  79.3 35.7 %copy-start = (f32[1,3]{1,0:T(1,128)S(1)}, f32[1,3]{1,0:T(1,128)}, u32[]{:S(2)}) copy-start(f32[1,3]{1,0:T(1,128)} %drift_ref.1) | copy-start | bytes 40
  79.3 17.5 %collective-permute-start.3 = (f32[3,2,72,256]{3,2,1,0:T(8,128)S(1)}, f32[3,2,72,256]{3,2,1,0:T(8,128)S(1)}, u32[]{:S(2)}, u32[]{:S(2)}) collective-permute-start(f32[3,2,72,256]{3,2,1,0:T(8,128)S(1)} %get-tuple-element.53), channel_id=1, source_target_pairs={{1,0},{2,1},{3,2},{4,3},{5,4},{6,5},{7,6},{8,7},{9,8},{10,9},{11,1... | collective-permute-start | bytes 1327112 | tf_op jit(solution)/shard_map/ppermute | solution.py:606
  117.4 24.4 %collective-permute-start.6 = (f32[3,3,64,256]{3,2,1,0:T(8,128)S(1)}, f32[3,3,64,256]{3,2,1,0:T(8,128)S(1)}, u32[]{:S(2)}, u32[]{:S(2)}) collective-permute-start(f32[3,3,64,256]{3,2,1,0:T(8,128)S(1)} %get-tuple-element.45), channel_id=1, source_target_pairs={{0,1},{1,2},{2,3},{3,4},{4,5},{5,6},{6,7},{7,8},{8,9},{9,10},{10,1... | collective-permute-start | bytes 1769480 | tf_op jit(solution)/shard_map/ppermute | solution.py:601
  122.3 19.5 %collective-permute-start.8 = (f32[3,3,64,256]{3,2,1,0:T(8,128)S(1)}, f32[3,3,64,256]{3,2,1,0:T(8,128)S(1)}, u32[]{:S(2)}, u32[]{:S(2)}) collective-permute-start(f32[3,3,64,256]{3,2,1,0:T(8,128)S(1)} %get-tuple-element.47), channel_id=1, source_target_pairs={{1,0},{2,1},{3,2},{4,3},{5,4},{6,5},{7,6},{8,7},{9,8},{10,9},{11,1... | collective-permute-start | bytes 1769480 | tf_op jit(solution)/shard_map/ppermute | solution.py:606
  122.3 3.5 %collective-permute-start.4 = (f32[72,256]{1,0:T(8,128)S(1)}, f32[72,256]{1,0:T(8,128)S(1)}, u32[]{:S(2)}, u32[]{:S(2)}) collective-permute-start(f32[72,256]{1,0:T(8,128)S(1)} %get-tuple-element.42), channel_id=1, source_target_pairs={{32,0},{64,32},{96,64},{0,96},{33,1},{65,33},{97,65},{1,97},{34,2}... | collective-permute-start | bytes 221192 | tf_op jit(solution)/shard_map/ppermute | solution.py:606
  123.1 5.0 %collective-permute-start.5 = (f32[72,256]{1,0:T(8,128)S(1)}, f32[72,256]{1,0:T(8,128)S(1)}, u32[]{:S(2)}, u32[]{:S(2)}) collective-permute-start(f32[72,256]{1,0:T(8,128)S(1)} %get-tuple-element.43), channel_id=1, source_target_pairs={{0,32},{32,64},{64,96},{96,0},{1,33},{33,65},{65,97},{97,1},{2,34}... | collective-permute-start | bytes 221192 | tf_op jit(solution)/shard_map/ppermute | solution.py:601
  128.1 8.0 %collective-permute-start.7 = (f32[3,3,8,256]{3,2,1,0:T(8,128)S(1)}, f32[3,3,8,256]{3,2,1,0:T(8,128)S(1)}, u32[]{:S(2)}, u32[]{:S(2)}) collective-permute-start(f32[3,3,8,256]{3,2,1,0:T(8,128)S(1)} %get-tuple-element.46), channel_id=1, source_target_pairs={{0,1},{1,2},{2,3},{3,4},{4,5},{5,6},{6,7},{7,8},{8,9},{9,10},{10,1... | collective-permute-start | bytes 221192 | tf_op jit(solution)/shard_map/ppermute | solution.py:601
  134.7 7.1 %collective-permute-start.9 = (f32[3,3,8,256]{3,2,1,0:T(8,128)S(1)}, f32[3,3,8,256]{3,2,1,0:T(8,128)S(1)}, u32[]{:S(2)}, u32[]{:S(2)}) collective-permute-start(f32[3,3,8,256]{3,2,1,0:T(8,128)S(1)} %get-tuple-element.48), channel_id=1, source_target_pairs={{1,0},{2,1},{3,2},{4,3},{5,4},{6,5},{7,6},{8,7},{9,8},{10,9},{11,1... | collective-permute-start | bytes 221192 | tf_op jit(solution)/shard_map/ppermute | solution.py:606
  143.2 6.2 %collective-permute-start.10 = (f32[112,128]{1,0:T(8,128)S(1)}, f32[112,128]{1,0:T(8,128)S(1)}, u32[]{:S(2)}, u32[]{:S(2)}) collective-permute-start(f32[112,128]{1,0:T(8,128)S(1)} %shard_map.54), channel_id=1, source_target_pairs={{0,128},{1,129},{2,130},{3,131},{4,132},{5,133},{6,134},{7,135},{8... | collective-permute-start | bytes 172040 | tf_op jit(solution)/shard_map/ppermute | solution.py:652
